TPU v7x, 32 devices: a whole 2x2x4 slice. The times are simulated.
32 devices in a mesh: facet: 4 (over z), sub: 2 (over y), wa: 4 (over x, core).
Axes of the slice: x: 2, y: 2, z: 4, core: 2. Of those that a mesh axis runs over, the one named last changes fastest.
Arguments:
- facet_data: bfloat16 [4, 128, 2, 8192], P('facet', ('sub', 'wa')), may hold values from -6 to 6
- window: float32 [8192], replicated, may hold values from 0.1 to 1
- screen_phase: float32 [1024, 1024], P('facet'), may hold values from -0.5 to 0.5
- facet_shift: int32 [4], replicated, may hold values from 0 to 1023
- sub_offset: int32 [8], replicated, may hold values from 0 to 8191
- win_start: int32 [4, 8], replicated, may hold values from 0 to 512
- win_extent: int32 [4, 8], replicated, may hold values from 256 to 512, as said below
- owner_slot: int32 [8], replicated, may hold values from 0 to 7, each once
- layer_w: int32 [8], replicated, may hold values from -12 to 12
Outputs:
- layers: bfloat16 [8, 8, 1024, 2, 1024], P('sub', 'wa', 'facet')
Inputs may be any that keep to these rules, and one draw needn't show every extreme that they name: win_start[f, j] + win_extent[f, j] <= 1024 for every facet f and subgrid j. A permutation of the subgrids; the subgrid with owner_slot = p belongs to sub index p // 4.
All inputs are finite; a program needn't handle non-finite values.
Results may differ from a plain program's by a relative error of at most 0.008.
Values may be sent and summed in bfloat16 or wider, within the bound.
A program may use at most 128 MiB of HBM per device.

v0:
```python
import functools
import math

import jax
import jax.numpy as jnp
import numpy as np
from jax import lax
from jax.experimental import pallas as pl
from jax.experimental.pallas import tpu as pltpu
from jax.sharding import PartitionSpec as P

RADIX = 4


def table(products, modulus, sign_value):
    angles = (sign_value * 2.0 * math.pi / modulus) * (products % modulus).astype(np.float64)
    return np.cos(angles), np.sin(angles)


def wave(products, modulus):
    angles = (2.0 * math.pi / modulus) * (products % modulus).astype(jnp.float32)
    return jnp.cos(angles), jnp.sin(angles)


def high(form, left, right):
    return jnp.einsum(form, left, right, precision=lax.Precision.HIGH)


def facet_spectrum(signal):
    strip_rows = signal.shape[0]
    facet_len = signal.shape[2]
    inner_len = 128
    outer_len = facet_len // inner_len
    grid_in = signal.reshape(strip_rows, 2 * outer_len, inner_len)
    outer_ids = np.arange(outer_len)
    inner_ids = np.arange(inner_len)
    c1, s1 = table(outer_ids[:, None] * outer_ids[None, :], outer_len, -1.0)
    first = np.block([[c1, -s1], [s1, c1]]).astype(np.float32)
    mid = high("zy,ryq->rzq", jnp.asarray(first), grid_in)
    mid_real = mid[:, :outer_len]
    mid_imag = mid[:, outer_len:]
    ct, st = table(outer_ids[:, None] * inner_ids[None, :], facet_len, -1.0)
    ct = jnp.asarray(ct.astype(np.float32))
    st = jnp.asarray(st.astype(np.float32))
    turned_real = mid_real * ct - mid_imag * st
    turned_imag = mid_real * st + mid_imag * ct
    turned = jnp.concatenate([turned_real, turned_imag], 2)
    c2, s2 = table(inner_ids[:, None] * inner_ids[None, :], inner_len, -1.0)
    scale = 1.0 / math.sqrt(facet_len)
    second = (np.block([[c2, s2], [-s2, c2]]) * scale).astype(np.float32)
    out = high("rpn,nq->rqp", turned, jnp.asarray(second))
    return out.reshape(strip_rows, 2, facet_len)


def finish_kernel(band, count, scale_rows, left_ref, right_ref, cos_ref, sin_ref, fwd_ref, out_ref, held):
    layer = pl.program_id(1)
    grid_size = cos_ref.shape[2]
    part = grid_size // RADIX

    @pl.when(layer == 0)
    def _():
        rows = jnp.dot(left_ref[...], right_ref[...], preferred_element_type=jnp.float32)
        held[...] = (rows * scale_rows).astype(jnp.bfloat16)

    real = held[:band, :].astype(jnp.float32)
    imag = held[band:, :].astype(jnp.float32)
    cos = cos_ref[0]
    sin = sin_ref[0]
    s_real = (real * cos - imag * sin).astype(jnp.bfloat16)
    s_imag = (real * sin + imag * cos).astype(jnp.bfloat16)
    pieces = []
    for p in range(RADIX):
        lo, hi = p * part, (p + 1) * part
        pair = jnp.concatenate([s_real[:, lo:hi], s_imag[:, lo:hi]], 1)
        got = jnp.dot(pair, fwd_ref[p], preferred_element_type=jnp.float32)
        pieces.append((got[:, :part], got[:, part:]))
    (ar, ai), (br, bi), (cr, ci), (dr, di) = pieces
    er, ei, fr, fi = ar + cr, ai + ci, ar - cr, ai - ci
    gr, gi, hr, hi_ = br + dr, bi + di, br - dr, bi - di
    reals = jnp.concatenate([er + gr, fr + hi_, er - gr, fr - hi_], 1)
    imags = jnp.concatenate([ei + gi, fi - hr, ei - gi, fi + hr], 1)
    out_ref[0, 0, :, 0, :] = reals.astype(jnp.bfloat16)
    out_ref[0, 0, :, 1, :] = imags.astype(jnp.bfloat16)


def finish(left, right, cos, sin, forward, slots, scale_rows):
    layers, band, grid_size = cos.shape
    count = right.shape[0]
    return pl.pallas_call(
        functools.partial(finish_kernel, band, count, scale_rows),
        grid=(slots, layers),
        out_shape=jax.ShapeDtypeStruct((slots, layers, band, 2, grid_size), jnp.bfloat16),
        in_specs=[
            pl.BlockSpec((2 * band, count), lambda s, l: (0, 0)),
            pl.BlockSpec((count, grid_size), lambda s, l: (0, s)),
            pl.BlockSpec((1, band, grid_size), lambda s, l: (l, 0, 0)),
            pl.BlockSpec((1, band, grid_size), lambda s, l: (l, 0, 0)),
            pl.BlockSpec(forward.shape, lambda s, l: (0, 0, 0)),
        ],
        out_specs=pl.BlockSpec((1, 1, band, 2, grid_size), lambda s, l: (s, l, 0, 0, 0)),
        scratch_shapes=[pltpu.VMEM((2 * band, grid_size), jnp.bfloat16)],
        compiler_params=pltpu.CompilerParams(vmem_limit_bytes=48 * 1024 * 1024),
        cost_estimate=pl.CostEstimate(flops=10_000_000_000, bytes_accessed=20_000_000, transcendentals=0),
    )(left, right, cos, sin, forward)


def doubled(block, axis, size, steps):
    order = [0]
    for step in steps:
        other = lax.ppermute(block, axis, [(i, i ^ step) for i in range(size)])
        block = jnp.concatenate([block, other], 0)
        order = order + [o ^ step for o in order]
    return block, order


def local(
    facet_data,
    window,
    screen_phase,
    facet_shift,
    sub_offset,
    win_start,
    win_extent,
    owner_slot,
    layer_w,
):
    facets = lax.axis_size("facet")
    owners = lax.axis_size("sub")
    teams = lax.axis_size("wa")
    facet_id = lax.axis_index("facet")
    team_id = lax.axis_index("wa")
    strip_rows = facet_data.shape[1]
    facet_len = facet_data.shape[3]
    band = screen_phase.shape[0]
    grid_size = screen_phase.shape[1]
    width = grid_size // 2
    part = grid_size // RADIX
    total_subs = owner_slot.shape[0]
    slots = total_subs // owners
    share = strip_rows // facets
    strip_total = strip_rows * owners * teams

    spectrum = facet_spectrum(facet_data[0].astype(jnp.float32) * window)
    slot_ids = jnp.arange(total_subs, dtype=jnp.int32)
    chooser = (owner_slot[None, :] == slot_ids[:, None]).astype(jnp.int32)
    offset_slot = jnp.sum(chooser * sub_offset[None, :], axis=1)
    start_all = jnp.sum(win_start[:, None, :] * chooser[None], axis=2)
    extent_all = jnp.sum(win_extent[:, None, :] * chooser[None], axis=2)
    start_mine = lax.dynamic_index_in_dim(start_all, facet_id, 0, keepdims=False)
    extent_mine = lax.dynamic_index_in_dim(extent_all, facet_id, 0, keepdims=False)
    shift_value = lax.dynamic_index_in_dim(facet_shift, facet_id, 0, keepdims=False)
    begin = (offset_slot + start_mine) % facet_len
    steps = jnp.arange(width, dtype=jnp.int32)
    turn_cos, turn_sin = wave(shift_value * (start_mine[:, None] + steps[None, :]), grid_size)
    inside = steps[None, :] < extent_mine[:, None]
    turn_cos = jnp.where(inside, turn_cos, 0.0)
    turn_sin = jnp.where(inside, turn_sin, 0.0)
    wrapped = jnp.concatenate([spectrum, spectrum[:, :, :width]], 2)
    cuts = []
    for j in range(total_subs):
        picked = lax.dynamic_slice_in_dim(wrapped, begin[j], width, 2)
        cos_j = turn_cos[j][None, :]
        sin_j = turn_sin[j][None, :]
        cuts.append(
            jnp.concatenate(
                [
                    picked[:, 0] * cos_j - picked[:, 1] * sin_j,
                    picked[:, 0] * sin_j + picked[:, 1] * cos_j,
                ],
                1,
            ).astype(jnp.bfloat16)
        )
    sendable = jnp.stack(cuts).reshape(owners, slots, facets, share, 2 * width)
    sendable = sendable.transpose(2, 0, 1, 3, 4).reshape(facets * owners, slots * share, 2 * width)
    received = lax.all_to_all(sendable, ("facet", "sub"), split_axis=0, concat_axis=0, tiled=True)

    v_ids = np.arange(part)[None, :] * RADIX + np.arange(RADIX)[:, None]
    back_cos, back_sin = table(np.arange(width)[:, None] * v_ids.reshape(1, -1), grid_size, 1.0)
    back = np.block([[back_cos, back_sin], [-back_sin, back_cos]])
    moved = jnp.dot(
        received.reshape(facets * owners * slots * share, 2 * width),
        jnp.asarray(back.astype(jnp.bfloat16)),
        preferred_element_type=jnp.float32,
    ).reshape(facets, owners, slots, share, 2, grid_size)
    my_slot = lax.axis_index("sub") * slots
    start_slot = lax.dynamic_slice_in_dim(start_all, my_slot, slots, 1)
    ramp_cos, ramp_sin = wave(
        start_slot[:, :, None] * jnp.asarray(v_ids.reshape(1, 1, -1).astype(np.int32)), grid_size
    )
    scale_col = 1.0 / math.sqrt(facets * grid_size)
    ramp_cos = (ramp_cos * scale_col)[:, None, :, None, :]
    ramp_sin = (ramp_sin * scale_col)[:, None, :, None, :]
    col_real = jnp.sum(moved[:, :, :, :, 0] * ramp_cos - moved[:, :, :, :, 1] * ramp_sin, 0)
    col_imag = jnp.sum(moved[:, :, :, :, 0] * ramp_sin + moved[:, :, :, :, 1] * ramp_cos, 0)
    image = jnp.stack([col_real, col_imag], 0).astype(jnp.bfloat16)
    image = image.transpose(0, 1, 3, 2, 4).reshape(2 * owners * share, slots * grid_size)
    facet_steps = [1 << i for i in range(facets.bit_length() - 1)]
    team_steps = [1 << i for i in range(teams.bit_length() - 1)][::-1]
    right, facet_order = doubled(image, "facet", facets, facet_steps)
    right, team_order = doubled(right, "wa", teams, team_steps)

    me_f, me_t, t_ids, f_ids, c_ids, o_ids, r_ids = np.meshgrid(
        np.arange(facets), np.arange(teams), np.array(team_order), np.array(facet_order),
        np.arange(2), np.arange(owners), np.arange(share), indexing="ij"
    )
    global_row = (o_ids * teams + (t_ids ^ me_t)) * strip_rows + (f_ids ^ me_f) * share + r_ids
    global_row = global_row.reshape(facets, teams, 1, -1)
    is_imag = c_ids.reshape(facets, teams, 1, -1)
    my_rows = np.arange(grid_size).reshape(facets, 1, band, 1)
    all_cos, all_sin = table(my_rows * global_row, grid_size, -1.0)
    real_rows = np.where(is_imag == 1, -all_sin, all_cos)
    imag_rows = np.where(is_imag == 1, all_cos, all_sin)
    left_all = np.concatenate([real_rows, imag_rows], 2).astype(jnp.bfloat16)
    left_all = left_all.reshape(facets * teams, 2 * band, -1)
    left = lax.dynamic_index_in_dim(jnp.asarray(left_all), facet_id * teams + team_id, 0, keepdims=False)

    layer_dev = layer_w.shape[0] // teams
    levels = lax.dynamic_slice_in_dim(layer_w, team_id * layer_dev, layer_dev, 0)
    pick = np.zeros((grid_size, grid_size), np.float32)
    pick[v_ids.reshape(-1), np.arange(grid_size)] = 1.0
    ordered = jnp.dot(
        screen_phase,
        jnp.asarray(pick.astype(jnp.bfloat16)).astype(jnp.float32),
        precision=lax.Precision.HIGHEST,
    )
    angles = levels.astype(jnp.float32)[:, None, None] * ordered[None]
    cos = jnp.cos(angles)
    sin = jnp.sin(angles)

    fwd_cos, fwd_sin = table(v_ids[:, :, None] * np.arange(part)[None, None, :], grid_size, -1.0)
    rounded = lambda x: x.astype(jnp.bfloat16).astype(np.float64)
    fwd_cos, fwd_sin = rounded(fwd_cos), rounded(fwd_sin)
    forward = np.concatenate(
        [np.concatenate([fwd_cos, fwd_sin], 2), np.concatenate([-fwd_sin, fwd_cos], 2)], 1
    )
    forward = (forward / math.sqrt(grid_size)).astype(jnp.bfloat16)
    return finish(left, right, cos, sin, jnp.asarray(forward), slots, 1.0 / math.sqrt(strip_total))


def solution(mesh):
    in_specs = (
        P("facet", ("sub", "wa"), None, None),
        P(),
        P("facet", None),
        P(),
        P(),
        P(),
        P(),
        P(),
        P(),
    )
    out_specs = P("sub", "wa", "facet", None, None)
    return jax.shard_map(local, mesh=mesh, in_specs=in_specs, out_specs=out_specs, check_vma=False)
```

profile of v0, /device:TPU:0, one launch (start us, length us, event | category | flops | bytes accessed | tf_op | source)
XLA Modules:
  0.0 103.8 jit_solution(16551782262880271299)
XLA Ops:
  0.8 0.8 select_reduce_fusion
  1.5 0.9 multiply_reduce_fusion
  13.1 1.3 %dynamic_slice.49 = s32[1]{0:T(128)} dynamic-slice(s32[4]{0:T(128)} %param.21, s32[]{:T(128)S(6)} %select_n.75), dynamic_slice_sizes={1} | dynamic-slice | bytes 12 | tf_op jit(solution)/shard_map/jit(dynamic_index_in_dim)/dynamic_slice | solution.py:151
  14.5 1.4 %reshape.1385 = f32[16,128,128]{2,1,0:T(8,128)S(1)} reshape(bf16[1,16,2,8192]{3,2,1,0:T(2,128)(2,1)} %param.18) | data formatting | bytes 1572864 | tf_op jit(solution)/shard_map/convert_element_type | solution.py:143
  16.6 1.5 %convolution_bitcast_fusion.2 = f32[16,128,128]{2,1,0:T(8,128)S(1)} fusion(f32[128,128,1]{1,0,2:T(8,128)} %constant.112, f32[16,128,128]{2,1,0:T(8,128)S(1)} %reshape.1385, f32[128,128]{1,0:T(8,128)S(1)} %bitcast.283), kind=kOutput, calls=%fused_computation.12 | convolution fusion | flops 201588736 | bytes 2228224 | tf_op jit(solution)/shard_map/zy,ryq->rzq/dot_general | solution.py:26
  18.3 1.6 %convolution_bitcast_fusion.1 = f32[16,256,64]{1,2,0:T(8,128)} fusion(f32[256,256,1]{1,0,2:T(8,128)S(1)} %copy-done.2, f32[16,64,128]{2,1,0:T(8,128)S(1)} %get-tuple-element.20, f32[16,64,128]{2,1,0:T(8,128)S(1)} %get-tuple-element.19), kind=kOutput, calls=%fused_computation.11 | convolution fusion | flops 402915328 | bytes 2359296 | tf_op jit(solution)/shard_map/rpn,nq->rqp/dot_general | solution.py:26
  19.9 1.8 %copy.65 = f32[16,256,64]{2,1,0:T(8,128)S(1)} copy(f32[16,256,64]{1,2,0:T(8,128)} %convolution_bitcast_fusion.1) | data formatting | bytes 2097152 | tf_op jit(solution)/shard_map/rpn,nq->rqp/transpose | solution.py:26
  21.7 2.0 %reshape.1381 = f32[16,2,8192]{2,1,0:T(2,128)} reshape(f32[16,256,64]{2,1,0:T(8,128)S(1)} %copy.65) | data formatting | bytes 2097152 | tf_op jit(solution)/shard_map/reshape | solution.py:52
  23.7 0.8 slice.248
  29.6 0.8 cosine_select_fusion
  30.4 2.5 %fusion.7 = (f32[16,2,512]{2,1,0:T(2,128)S(1)}, f32[16,2,512]{2,1,0:T(2,128)S(1)}, f32[16,2,512]{2,1,0:T(2,128)S(1)}, f32[16,2,512]{2,1,0:T(2,128)S(1)}, f32[16,...) fusion(s32[]{:T(128)S(6)} %select_n.87, ...), kind=kLoop, calls=%fused_computation.36 | loop fusion | flops 131072 | bytes 1638432 | tf_op jit(solution)/shard_map/concatenate | solution.py:158
  34.7 7.3 %all-to-all-start = ((bf16[8,16,1024]{2,1,0:T(8,128)(2,1)}), bf16[8,16,1024]{2,1,0:T(8,128)(2,1)S(1)}, u32[]{:S(2)}, u32[]{:S(2)}) async-start(bf16[8,16,1024]{2,1,0:T(8,128)(2,1)} %reshape.1383), calls=%async_computation | async-start | bytes 524288 | tf_op jit(solution)/shard_map/all_to_all | solution.py:175
  42.7 8.2 %all-to-all-done = bf16[8,16,1024]{2,1,0:T(8,128)(2,1)S(1)} async-done(((bf16[8,16,1024]{2,1,0:T(8,128)(2,1)}), bf16[8,16,1024]{2,1,0:T(8,128)(2,1)S(1)}, u32[]{:S(2)}, u32[]{:S(2)}) %all-to-all-start) | async-done | bytes 262176 | tf_op jit(solution)/shard_map/all_to_all | solution.py:175
  51.0 3.9 %fusion.5 = f32[4,2,4,4,2,1024]{5,3,4,2,1,0:T(4,128)S(1)} fusion(bf16[2,1024,1024,1,1,1]{2,1,0,5,4,3:T(8,128)(2,1)} %constant.114, bf16[4,2,4,4,1024,1]{4,3,2,1,0,5:T(4,128)(2,1)S(1)} %reshape.1388), kind=kOutput, calls=%fused_computation.28 | convolution fusion | flops 536870912 | bytes 5505024 | tf_op jit(solution)/shard_map/dot_general | solution.py:180
  55.6 1.1 %collective-permute-start = (bf16[16,4096]{1,0:T(8,128)(2,1)S(1)}, bf16[16,4096]{1,0:T(8,128)(2,1)S(1)}, u32[]{:S(2)}, u32[]{:S(2)}) collective-permute-start(bf16[16,4096]{1,0:T(8,128)(2,1)S(1)} %bitcast.276), channel_id=1, source_target_pairs={{0,8},{8,0},{16,24},{24,16},{1,9},{9,1},{17,25},{25,17},{2,10},{10... | collective-permute-start | bytes 393224 | tf_op jit(solution)/shard_map/ppermute | solution.py:110
  56.7 2.5 %convolution_bitcast_fusion = f32[256,1024]{0,1:T(8,128)S(1)} fusion(bf16[1024,1024]{1,0:T(8,128)(2,1)S(1)} %copy-done.1, f32[256,1024]{1,0:T(8,128)S(1)} %copy-done), kind=kOutput, calls=%fused_computation.10 | convolution fusion | flops 3221225472 | bytes 4194304 | tf_op jit(solution)/shard_map/dot_general | solution.py:221
  60.7 1.1 %collective-permute-start.1 = (bf16[32,4096]{1,0:T(8,128)(2,1)S(1)}, bf16[32,4096]{1,0:T(8,128)(2,1)S(1)}, u32[]{:S(2)}, u32[]{:S(2)}) collective-permute-start(bf16[32,4096]{1,0:T(8,128)(2,1)S(1)} %pad_maximum_fusion.2), channel_id=1, source_target_pairs={{0,16},{8,24},{16,0},{24,8},{1,17},{9,25},{17,1},{25,9},{2,18},{10... | collective-permute-start | bytes 786440 | tf_op jit(solution)/shard_map/ppermute | solution.py:110
  61.8 8.6 %multiply_sine_fusion = (f32[2,256,1024]{2,1,0:T(8,128)}, f32[2,256,1024]{2,1,0:T(8,128)S(1)}) fusion(f32[256,1024]{1,0:T(8,128)S(1)} %copy.77, f32[2]{0:T(128)S(1)} %dynamic-slice_convert_fusion), kind=kLoop, calls=%fused_computation | loop fusion | flops 524288 | bytes 5242888 | tf_op jit(solution)/shard_map/sin | solution.py:228
  70.4 2.2 %collective-permute-done.1 = bf16[32,4096]{1,0:T(8,128)(2,1)S(1)} collective-permute-done((bf16[32,4096]{1,0:T(8,128)(2,1)S(1)}, bf16[32,4096]{1,0:T(8,128)(2,1)S(1)}, u32[]{:S(2)}, u32[]{:S(2)}) %collective-permute-start.1) | collective-permute-done | bytes 262176 | tf_op jit(solution)/shard_map/ppermute | solution.py:110
  72.6 1.6 %collective-permute-start.2 = (bf16[64,4096]{1,0:T(8,128)(2,1)S(1)}, bf16[64,4096]{1,0:T(8,128)(2,1)S(1)}, u32[]{:S(2)}, u32[]{:S(2)}) collective-permute-start(bf16[64,4096]{1,0:T(8,128)(2,1)S(1)} %pad_maximum_fusion.1), channel_id=1, source_target_pairs={{0,2},{1,3},{2,0},{3,1},{4,6},{5,7},{6,4},{7,5},{8,10},{9,11},{10,... | collective-permute-start | bytes 1572872 | tf_op jit(solution)/shard_map/ppermute | solution.py:110
  74.2 1.0 dynamic-slice_bitcast_fusion.left_ref
  75.2 10.4 %collective-permute-done.2 = bf16[64,4096]{1,0:T(8,128)(2,1)S(1)} collective-permute-done((bf16[64,4096]{1,0:T(8,128)(2,1)S(1)}, bf16[64,4096]{1,0:T(8,128)(2,1)S(1)}, u32[]{:S(2)}, u32[]{:S(2)}) %collective-permute-start.2) | collective-permute-done | bytes 524320 | tf_op jit(solution)/shard_map/ppermute | solution.py:110
  85.8 2.6 %collective-permute-done.3 = bf16[128,4096]{1,0:T(8,128)(2,1)S(1)} collective-permute-done((bf16[128,4096]{1,0:T(8,128)(2,1)S(1)}, bf16[128,4096]{1,0:T(8,128)(2,1)S(1)}, u32[]{:S(2)}, u32[]{:S(2)}) %collective-permute-start.3) | collective-permute-done | bytes 1048608 | tf_op jit(solution)/shard_map/ppermute | solution.py:110
  88.5 15.3 %shard_map.172 = bf16[4,2,256,2,1024]{4,3,2,1,0:T(2,128)(2,1)} custom-call(bf16[512,256]{1,0:T(8,128)(2,1)S(1)} %dynamic-slice_bitcast_fusion.left_ref, bf16[256,4096]{1,0:T(8,128)(2,1)S(1)} %constant_dynamic-update-slice_fusion.right_ref, f32[2,256,1024]{2,1,0:T(8,128)S(1)} %get-tuple-element.22.cos_ref, f32[2,256,1024]{2,1,0:T(8,128)} %get-tuple-element.21.sin_ref, ...), custom_call_target="tpu_custom_call" | custom-call | flops 10000000000 | bytes 20000000 | tf_op jit(solution)/shard_map/pallas_call | solution.py:89
  (63 shorter events, 7.2 us)
Async XLA Ops:
  0.0 56.7 %copy-start = (f32[256,1024]{1,0:T(8,128)S(1)}, f32[256,1024]{1,0:T(8,128)}, u32[]{:S(2)}) copy-start(f32[256,1024]{1,0:T(8,128)} %param.20) | copy-start | bytes 3145732
  0.0 18.1 %copy-start.3 = (f32[64,128]{1,0:T(8,128)S(1)}, f32[64,128]{1,0:T(8,128)}, u32[]{:S(2)}) copy-start(f32[64,128]{1,0:T(8,128)} %constant.101.clone) | copy-start | bytes 98308
  0.0 18.1 %copy-start.4 = (f32[64,128]{1,0:T(8,128)S(1)}, f32[64,128]{1,0:T(8,128)}, u32[]{:S(2)}) copy-start(f32[64,128]{1,0:T(8,128)} %constant.100.clone) | copy-start | bytes 98308
  16.6 1.7 %copy-start.2 = (f32[256,256,1]{1,0,2:T(8,128)S(1)}, f32[256,256,1]{1,0,2:T(8,128)}, u32[]{:S(2)}) copy-start(f32[256,256,1]{1,0,2:T(8,128)} %constant.113) | copy-start | bytes 786436
  33.2 8.9 %copy-start.5 = (s32[1024]{0:T(1024)S(1)}, s32[1024]{0:T(1024)}, u32[]{:S(2)}) copy-start(s32[1024]{0:T(1024)} %constant.111) | copy-start | bytes 12292
  34.7 16.2 %all-to-all-start = ((bf16[8,16,1024]{2,1,0:T(8,128)(2,1)}), bf16[8,16,1024]{2,1,0:T(8,128)(2,1)S(1)}, u32[]{:S(2)}, u32[]{:S(2)}) async-start(bf16[8,16,1024]{2,1,0:T(8,128)(2,1)} %reshape.1383), calls=%async_computation | async-start | bytes 524288 | tf_op jit(solution)/shard_map/all_to_all | solution.py:175
  54.9 1.8 %copy-start.1 = (bf16[1024,1024]{1,0:T(8,128)(2,1)S(1)}, bf16[1024,1024]{1,0:T(8,128)(2,1)}, u32[]{:S(2)}) copy-start(bf16[1024,1024]{1,0:T(8,128)(2,1)} %constant.106.clone) | copy-start | bytes 6291460
  55.6 5.0 %collective-permute-start = (bf16[16,4096]{1,0:T(8,128)(2,1)S(1)}, bf16[16,4096]{1,0:T(8,128)(2,1)S(1)}, u32[]{:S(2)}, u32[]{:S(2)}) collective-permute-start(bf16[16,4096]{1,0:T(8,128)(2,1)S(1)} %bitcast.276), channel_id=1, source_target_pairs={{0,8},{8,0},{16,24},{24,16},{1,9},{9,1},{17,25},{25,17},{2,10},{10... | collective-permute-start | bytes 393224 | tf_op jit(solution)/shard_map/ppermute | solution.py:110
  59.2 0.7 copy-start.6
  60.7 11.9 %collective-permute-start.1 = (bf16[32,4096]{1,0:T(8,128)(2,1)S(1)}, bf16[32,4096]{1,0:T(8,128)(2,1)S(1)}, u32[]{:S(2)}, u32[]{:S(2)}) collective-permute-start(bf16[32,4096]{1,0:T(8,128)(2,1)S(1)} %pad_maximum_fusion.2), channel_id=1, source_target_pairs={{0,16},{8,24},{16,0},{24,8},{1,17},{9,25},{17,1},{25,9},{2,18},{10... | collective-permute-start | bytes 786440 | tf_op jit(solution)/shard_map/ppermute | solution.py:110
  72.6 13.0 %collective-permute-start.2 = (bf16[64,4096]{1,0:T(8,128)(2,1)S(1)}, bf16[64,4096]{1,0:T(8,128)(2,1)S(1)}, u32[]{:S(2)}, u32[]{:S(2)}) collective-permute-start(bf16[64,4096]{1,0:T(8,128)(2,1)S(1)} %pad_maximum_fusion.1), channel_id=1, source_target_pairs={{0,2},{1,3},{2,0},{3,1},{4,6},{5,7},{6,4},{7,5},{8,10},{9,11},{10,... | collective-permute-start | bytes 1572872 | tf_op jit(solution)/shard_map/ppermute | solution.py:110
  85.7 2.7 %collective-permute-start.3 = (bf16[128,4096]{1,0:T(8,128)(2,1)S(1)}, bf16[128,4096]{1,0:T(8,128)(2,1)S(1)}, u32[]{:S(2)}, u32[]{:S(2)}) collective-permute-start(bf16[128,4096]{1,0:T(8,128)(2,1)S(1)} %pad_maximum_fusion), channel_id=1, source_target_pairs={{0,1},{1,0},{2,3},{3,2},{4,5},{5,4},{6,7},{7,6},{8,9},{9,8},{10,11... | collective-permute-start | bytes 3145736 | tf_op jit(solution)/shard_map/ppermute | solution.py:110
where the time goes:
time: 105 us; the launch traced here: 104 us
  waiting for transfers between devices  24 us (23%)
  other arithmetic  16.1 us (15%)
  between operations  15.4 us (15%)
  Pallas kernels  15.3 us (15%)
  local copies, waits for them, and re-layouts  12.3 us (12%)
  starting transfers between devices  11.2 us (11%)
  matrix products  9.36 us (9%)
    ppermute x4, waiting for transfers between devices, doubled(): other = lax.ppermute(block, axis, [(i, i ^ step) for i in range(size)])  15.8 us
    pallas_call x1, Pallas kernels, finish(): pl.pallas_call(functools.partial(finish_kernel, band, count, scale_rows),...  15.3 us
    sin x1, other arithmetic, local(): sin = jnp.sin(angles)  8.62 us
    all_to_all x1, waiting for transfers between devices, local(): lax.all_to_all(sendable, ('facet', 'sub'), split_axis=0, concat_axis=0, t...  8.24 us
    all_to_all x1, starting transfers between devices, local(): lax.all_to_all(sendable, ('facet', 'sub'), split_axis=0, concat_axis=0, t...  7.32 us
    ppermute x4, starting transfers between devices, doubled(): other = lax.ppermute(block, axis, [(i, i ^ step) for i in range(size)])  3.88 us
    dot_general x1, matrix products, local(): jnp.dot(received.reshape(facets * owners * slots * share, 2 * width), jnp...  3.87 us
    dot_general x2, matrix products, high(): return jnp.einsum(form, left, right, precision=lax.Precision.HIGH)  3.02 us
  transfers between devices with their start and end apart: 5, of which 5 were waited for; matrix products, arithmetic and copies ran while one was open for 13% of the time, Pallas kernels for 0%

commit v1 on v0

v1 whole, which is shorter than its diff:
```python
import functools
import math

import jax
import jax.numpy as jnp
import numpy as np
from jax import lax
from jax.experimental import pallas as pl
from jax.experimental.pallas import tpu as pltpu
from jax.sharding import PartitionSpec as P

RADIX = 4
LANES = 128
PARTS = 2
MESH = pl.DeviceIdType.MESH


def table(products, modulus, sign_value):
    angles = (sign_value * 2.0 * math.pi / modulus) * (products % modulus).astype(np.float64)
    return np.cos(angles), np.sin(angles)


def sincos(angles):
    turns = jnp.floor(angles * (2.0 / math.pi) + 0.5)
    rest = angles - turns * 1.5703125
    rest = rest - turns * 4.837512969970703e-4
    rest = rest - turns * 7.549789948768648e-8
    square = rest * rest
    sine = rest + rest * square * (
        -1.6666654611e-1 + square * (8.3321608736e-3 + square * -1.9515295891e-4)
    )
    cosine = (1.0 - 0.5 * square) + square * square * (
        4.166664568298827e-2 + square * (-1.388731625493765e-3 + square * 2.443315711809948e-5)
    )
    quadrant = turns.astype(jnp.int32)
    odd = (quadrant & 1) == 1
    sin_size = jnp.where(odd, cosine, sine)
    cos_size = jnp.where(odd, sine, cosine)
    sin_value = jnp.where((quadrant & 2) == 2, -sin_size, sin_size)
    cos_value = jnp.where(((quadrant + 1) & 2) == 2, -cos_size, cos_size)
    return cos_value, sin_value


def strip_tables(facet_len, grid_size):
    inner_len = LANES
    outer_len = facet_len // inner_len
    outer_ids = np.arange(outer_len)
    inner_ids = np.arange(inner_len)
    c1, s1 = table(outer_ids[:, None] * outer_ids[None, :], outer_len, -1.0)
    first = np.block([[c1, -s1], [s1, c1]]).astype(jnp.bfloat16)
    ct, st = table(outer_ids[:, None] * inner_ids[None, :], facet_len, -1.0)
    twiddle = np.stack([ct, st]).astype(np.float32)
    fold = LANES // outer_len
    q_ids = (np.arange(inner_len // fold)[None, :] * fold + np.arange(fold)[:, None]).reshape(-1)
    c2, s2 = table(q_ids[:, None] * inner_ids[None, :], inner_len, -1.0)
    scale = 1.0 / math.sqrt(facet_len)
    second = (np.block([[c2, -s2], [s2, c2]]) * scale).astype(jnp.bfloat16)
    part = grid_size // RADIX
    v_ids = np.arange(part)[None, :] * RADIX + np.arange(RADIX)[:, None]
    bc, bs = table(np.arange(part)[None, :, None] * v_ids[:, None, :], grid_size, 1.0)
    back = np.concatenate([bc, bs], 2).astype(jnp.bfloat16)
    return first, twiddle, second, back


def column_kernel(
    dims,
    shift_ref,
    offset_ref,
    start_ref,
    extent_ref,
    slot_ref,
    level_ref,
    sig_ref,
    first_ref,
    twiddle_ref,
    second_ref,
    back_ref,
    phase_ref,
    gather_ref,
    cos_ref,
    sin_ref,
    mid,
    spec,
    turn,
    outgoing,
    incoming,
    wide,
    pack_send,
    pack_recv,
    plane_send,
    block_recv,
):
    facets, owners, teams, strip_rows, facet_len, grid_size, slots, total_subs = dims
    facet_id = lax.axis_index("facet")
    sub_id = lax.axis_index("sub")
    team_id = lax.axis_index("wa")
    group = facets // slots
    chunk = strip_rows // group
    width = grid_size // 2
    part = grid_size // RADIX
    cores = 2
    spread = teams // cores
    core_id = lax.rem(team_id, cores)
    sibling = team_id + 1 - 2 * core_id

    def team_at(step):
        return lax.rem(team_id + cores * step, teams)

    barrier = pltpu.get_barrier_semaphore()
    peers = 0
    for off in range(facets):
        for turn_o in range(owners):
            if off or turn_o:
                pl.semaphore_signal(
                    barrier,
                    inc=1,
                    device_id=(lax.rem(facet_id + off, facets), lax.rem(sub_id + turn_o, owners), team_id),
                    device_id_type=MESH,
                )
                peers += 1
    for step in range(1, spread):
        pl.semaphore_signal(
            barrier, inc=1, device_id=(facet_id, sub_id, team_at(step)), device_id_type=MESH
        )
        peers += 1
    pl.semaphore_signal(barrier, inc=1, device_id=(facet_id, sub_id, sibling), device_id_type=MESH)
    peers += 1

    def holder(slot):
        def look(j, found):
            return jnp.where(slot_ref[j] == slot, j, found)

        return lax.fori_loop(0, total_subs, look, jnp.int32(0))

    outer_len = facet_len // LANES
    fold = LANES // outer_len
    tw_cos = twiddle_ref[0]
    tw_sin = twiddle_ref[1]

    def first_step(r, carry):
        got = jnp.dot(first_ref[...], sig_ref[r], preferred_element_type=jnp.float32)
        real, imag = got[:outer_len], got[outer_len:]
        rows = pl.ds(pl.multiple_of(r * outer_len, outer_len), outer_len)
        mid[rows, :LANES] = (real * tw_cos - imag * tw_sin).astype(jnp.bfloat16)
        mid[rows, LANES:] = (real * tw_sin + imag * tw_cos).astype(jnp.bfloat16)
        return carry

    lax.fori_loop(0, strip_rows, first_step, 0)
    tall = LANES // fold
    lane = lax.broadcasted_iota(jnp.int32, (tall, LANES), 1)

    def second_step(i, carry):
        rows = pl.ds(pl.multiple_of(i * LANES, LANES), LANES)
        got = lax.dot_general(
            second_ref[...], mid[rows, :], (((1,), (1,)), ((), ())), preferred_element_type=jnp.float32
        )
        for c in range(2):
            even = got[c * LANES : c * LANES + tall]
            odd = got[c * LANES + tall : (c + 1) * LANES]
            near = jnp.where(lane < outer_len, even, pltpu.roll(odd, outer_len, 1))
            far = jnp.where(lane < outer_len, pltpu.roll(even, outer_len, 1), odd)
            spec[c * tall : (c + 1) * tall, i * fold, :] = near
            spec[c * tall : (c + 1) * tall, i * fold + 1, :] = far
        return carry

    lax.fori_loop(0, strip_rows // fold, second_step, 0)

    held = [holder(p) for p in range(total_subs)]
    row_ids = lax.broadcasted_iota(jnp.int32, (total_subs, width), 0)
    k_ids = lax.broadcasted_iota(jnp.int32, (total_subs, width), 1)
    starts = jnp.zeros((total_subs, width), jnp.int32)
    extents = jnp.zeros((total_subs, width), jnp.int32)
    for p in range(total_subs):
        starts = jnp.where(row_ids == p, start_ref[facet_id, held[p]], starts)
        extents = jnp.where(row_ids == p, extent_ref[facet_id, held[p]], extents)
    product = (shift_ref[facet_id] * (starts + k_ids)) & (grid_size - 1)
    turn_cos, turn_sin = sincos(product.astype(jnp.float32) * (2.0 * math.pi / grid_size))
    inside = k_ids < extents
    turn_cos = jnp.where(inside, turn_cos, 0.0)
    turn_sin = jnp.where(inside, turn_sin, 0.0)
    for p in range(total_subs):
        turn[0, p] = turn_cos[p : p + 1]
        turn[1, p] = turn_sin[p : p + 1]

    pl.semaphore_wait(barrier, peers)

    wide_lane = lax.broadcasted_iota(jnp.int32, (strip_rows, LANES), 1)
    pieces = width // LANES
    my_slot = facet_id // group
    packs = []
    order = [s for s in range(slots // 2, slots)] + [s for s in range(slots // 2)][::-1]
    for step in order:
        for turn_o in list(range(1, owners)) + [0]:
            slot = lax.rem(my_slot + step, slots)
            owner = lax.rem(sub_id + turn_o, owners)
            p = owner * slots + slot
            j = holder(p)
            begin = lax.rem(offset_ref[j] + start_ref[facet_id, j], facet_len)
            q0 = lax.div(begin, LANES)
            shift = begin - q0 * LANES
            back_by = lax.rem(LANES - shift, LANES)
            tiles = []
            for c in range(2):
                rolled = []
                for q in range(pieces + 1):
                    tile = spec[c * tall + lax.rem(q0 + q, tall)]
                    rolled.append(pltpu.roll(tile, back_by, 1))
                tiles.append(
                    [jnp.where(wide_lane < LANES - shift, rolled[q], rolled[q + 1]) for q in range(pieces)]
                )
            reals, imags = [], []
            for q in range(pieces):
                lanes = slice(q * LANES, (q + 1) * LANES)
                cos = turn[0, p, :, lanes]
                sin = turn[1, p, :, lanes]
                reals.append(tiles[0][q] * cos - tiles[1][q] * sin)
                imags.append(tiles[0][q] * sin + tiles[1][q] * cos)
            block = jnp.concatenate(reals + imags, 1).astype(jnp.bfloat16)
            for g in range(group):
                target = slot * group + g
                piece = block[g * chunk : (g + 1) * chunk]
                n = len(packs)
                outgoing[n] = piece
                here = group == 1 and step == 0 and turn_o == 0
                if here:
                    incoming[facet_id, sub_id] = piece
                    packs.append((None, None))
                    continue
                copy = pltpu.make_async_remote_copy(
                    src_ref=outgoing.at[n],
                    dst_ref=incoming.at[facet_id, sub_id],
                    send_sem=pack_send.at[n],
                    recv_sem=pack_recv.at[facet_id, sub_id],
                    device_id=(target, owner, team_id),
                    device_id_type=MESH,
                )
                if step == 0 and turn_o == 0:
                    away = target != facet_id
                    pl.when(away)(copy.start)

                    @pl.when(target == facet_id)
                    def _():
                        incoming[facet_id, sub_id] = piece

                    packs.append((copy, away))
                else:
                    copy.start()
                    packs.append((copy, True))

    for p in range(RADIX):
        wide[p, :part] = back_ref[p]
        wide[p, part:, :part] = -back_ref[p][:, part:]
        wide[p, part:, part:] = back_ref[p][:, :part]
    mine = holder(sub_id * slots + my_slot)
    f_rows = lax.broadcasted_iota(jnp.int32, (facets, grid_size), 0)
    at = lax.broadcasted_iota(jnp.int32, (facets, grid_size), 1)
    v_ids = (at % part) * RADIX + at // part
    begins = jnp.zeros((facets, grid_size), jnp.int32)
    for f in range(facets):
        begins = jnp.where(f_rows == f, start_ref[f, mine], begins)
    ramp_cos, ramp_sin = sincos(
        ((begins * v_ids) & (grid_size - 1)).astype(jnp.float32) * (2.0 * math.pi / grid_size)
    )
    scale_col = 1.0 / math.sqrt(facets * grid_size)
    ramp_cos = ramp_cos * scale_col
    ramp_sin = ramp_sin * scale_col

    band = phase_ref.shape[0]
    block_v = LANES * RADIX
    from_ids = lax.broadcasted_iota(jnp.int32, (block_v, block_v), 0)
    to_ids = lax.broadcasted_iota(jnp.int32, (block_v, block_v), 1)
    chosen = (from_ids == (to_ids % LANES) * RADIX + to_ids // LANES).astype(jnp.float32).astype(jnp.bfloat16)
    for h in range(grid_size // block_v):
        whole = phase_ref[:, h * block_v : (h + 1) * block_v]
        ordered = jnp.zeros((band, block_v), jnp.float32)
        for level in range(3):
            digit = whole.astype(jnp.bfloat16)
            whole = whole - digit.astype(jnp.float32)
            ordered = ordered + jnp.dot(digit, chosen, preferred_element_type=jnp.float32)
        for p in range(RADIX):
            lanes = slice(p * part + h * LANES, p * part + (h + 1) * LANES)
            for l in range(cos_ref.shape[0]):
                level_value = level_ref[team_id * cos_ref.shape[0] + l].astype(jnp.float32)
                cos, sin = sincos(level_value * ordered[:, p * LANES : (p + 1) * LANES])
                cos_ref[l, :, lanes] = cos
                sin_ref[l, :, lanes] = sin

    for off in range(facets):
        for turn_o in range(owners):
            if off or turn_o:
                f = lax.rem(facet_id + off, facets)
                o = lax.rem(sub_id + turn_o, owners)
                pltpu.make_async_remote_copy(
                    src_ref=incoming.at[f, o],
                    dst_ref=incoming.at[f, o],
                    send_sem=pack_send.at[0],
                    recv_sem=pack_recv.at[f, o],
                    device_id=(f, o, team_id),
                    device_id_type=MESH,
                ).wait_recv()

    got = incoming[...].reshape(facets * owners * chunk, 2 * width).astype(jnp.float32)
    low_r, high_r = got[:, :part], got[:, part:width]
    low_i, high_i = got[:, width : width + part], got[:, width + part :]
    rows_f = owners * chunk
    images = [[], []]
    for p in range(RADIX):
        real, imag = [
            (low_r + high_r, low_i + high_i),
            (low_r - high_i, low_i + high_r),
            (low_r - high_r, low_i - high_i),
            (low_r + high_i, low_i - high_r),
        ][p]
        pair = jnp.concatenate([real.astype(jnp.bfloat16), imag.astype(jnp.bfloat16)], 1)
        moved = jnp.dot(pair, wide[p], preferred_element_type=jnp.float32)
        total_r = jnp.zeros((rows_f, part), jnp.float32)
        total_i = jnp.zeros((rows_f, part), jnp.float32)
        for f in range(facets):
            cos = ramp_cos[f : f + 1, p * part : (p + 1) * part]
            sin = ramp_sin[f : f + 1, p * part : (p + 1) * part]
            real = moved[f * rows_f : (f + 1) * rows_f, :part]
            imag = moved[f * rows_f : (f + 1) * rows_f, part:]
            total_r = total_r + (real * cos - imag * sin)
            total_i = total_i + (real * sin + imag * cos)
        images[0].append(total_r)
        images[1].append(total_i)
    for c in range(2):
        gather_ref[facet_id, team_id, c] = jnp.concatenate(images[c], 1).astype(jnp.bfloat16)

    def send(kind, f, team, h, target):
        return pltpu.make_async_remote_copy(
            src_ref=gather_ref.at[f, team, h],
            dst_ref=gather_ref.at[f, team, h],
            send_sem=plane_send.at[kind, f, team // cores, h],
            recv_sem=block_recv.at[f, team, h],
            device_id=target,
            device_id_type=MESH,
        )

    def arrive(f, team, h):
        send(0, f, team, h, (facet_id, sub_id, team_id)).wait_recv()

    has_next = facet_id < facets - 1
    has_last = facet_id > 0
    below = jnp.maximum(facet_id - 1, 0)
    above = jnp.minimum(facet_id + 1, facets - 1)

    def along(f, h, up, act):
        if up is None or up:

            @pl.when(has_next)
            def _():
                act(send(0, f, team_id, h, (above, sub_id, team_id)))

        if up is None or not up:

            @pl.when(has_last)
            def _():
                act(send(0 if up is not None else 1, f, team_id, h, (below, sub_id, team_id)))

        for step in range(1, spread):
            act(send(1 + step, f, team_id, h, (facet_id, sub_id, team_at(step))))
        act(send(1 + spread, f, team_id, h, (facet_id, sub_id, sibling)))

    def aside(f, team, h, act):
        act(send(1 + spread, f, team, h, (facet_id, sub_id, sibling)))

    def start(copy):
        copy.start()

    def finish_send(copy):
        copy.wait_send()

    def guarded(condition, body):
        if condition is None:
            body()
        else:
            pl.when(condition)(body)

    def sides(d):
        yield True, facet_id >= d, jnp.maximum(facet_id - d, 0)
        yield False, facet_id < facets - d, jnp.minimum(facet_id + d, facets - 1)

    def partners(d, h):
        for step in range(1, spread):
            if d == 0:
                arrive(facet_id, team_at(step), h)
                aside(facet_id, team_at(step), h, start)
            else:
                for _, condition, f in sides(d):

                    def body(f=f, step=step):
                        arrive(f, team_at(step), h)
                        aside(f, team_at(step), h, start)

                    pl.when(condition)(body)

    for h in range(PARTS):
        along(facet_id, h, None, start)
    for d in range(1, facets):
        for h in range(PARTS):
            for up, condition, f in sides(d):

                def body(f=f, h=h, up=up):
                    arrive(f, team_id, h)
                    along(f, h, up, start)

                pl.when(condition)(body)
            partners(d - 1, h)
    for h in range(PARTS):
        partners(facets - 1, h)
    for off in range(facets):
        for h in range(PARTS):
            f = lax.rem(facet_id + off, facets)
            for step in range(spread):
                arrive(f, lax.rem(sibling + cores * step, teams), h)

    for h in range(PARTS):
        along(facet_id, h, None, finish_send)
        for step in range(1, spread):
            aside(facet_id, team_at(step), h, finish_send)
    for d in range(1, facets):
        for h in range(PARTS):
            for up, condition, f in sides(d):

                def body(f=f, h=h, up=up):
                    along(f, h, up, finish_send)
                    for step in range(1, spread):
                        aside(f, team_at(step), h, finish_send)

                pl.when(condition)(body)
    for copy, away in packs:
        if away is True:
            copy.wait_send()
        elif away is not None:
            pl.when(away)(copy.wait_send)


def column(scalars, sig, window_rows, tables, phase, dims, layers):
    facets, owners, teams, strip_rows, facet_len, grid_size, slots, total_subs = dims
    first, twiddle, second, back = [jnp.asarray(x) for x in tables]
    group = facets // slots
    chunk = strip_rows // group
    width = grid_size // 2
    part = grid_size // RADIX
    band = phase.shape[0]
    smem = pl.BlockSpec(memory_space=pltpu.SMEM)
    vmem = pl.BlockSpec(memory_space=pltpu.VMEM)
    blocks = (facets, teams, 2, owners * chunk, grid_size)
    spread = teams // 2
    return pl.pallas_call(
        functools.partial(column_kernel, dims),
        out_shape=[
            jax.ShapeDtypeStruct(blocks, jnp.bfloat16),
            jax.ShapeDtypeStruct((layers, band, grid_size), jnp.float32),
            jax.ShapeDtypeStruct((layers, band, grid_size), jnp.float32),
        ],
        in_specs=[smem] * 6 + [vmem] * 6,
        out_specs=[vmem] * 3,
        scratch_shapes=[
            pltpu.VMEM((strip_rows * (facet_len // LANES), 2 * LANES), jnp.bfloat16),
            pltpu.VMEM((2 * facet_len // LANES, strip_rows, LANES), jnp.float32),
            pltpu.VMEM((2, total_subs, 1, width), jnp.float32),
            pltpu.VMEM((facets * owners, chunk, 2 * width), jnp.bfloat16),
            pltpu.VMEM((facets, owners, chunk, 2 * width), jnp.bfloat16),
            pltpu.VMEM((RADIX, 2 * part, 2 * part), jnp.bfloat16),
            pltpu.SemaphoreType.DMA((facets * owners,)),
            pltpu.SemaphoreType.DMA((facets, owners)),
            pltpu.SemaphoreType.DMA((2 + spread, facets, spread, PARTS)),
            pltpu.SemaphoreType.DMA((facets, teams, PARTS)),
        ],
        compiler_params=pltpu.CompilerParams(
            collective_id=0, has_side_effects=True, vmem_limit_bytes=48 * 1024 * 1024
        ),
        cost_estimate=pl.CostEstimate(flops=2_000_000_000, bytes_accessed=20_000_000, transcendentals=0),
    )(*scalars, sig, first, twiddle, second, back, phase)


def finish_kernel(band, scale_rows, left_ref, right_ref, cos_ref, sin_ref, fwd_ref, out_ref, held, wide, near, sem):
    layer = pl.program_id(1)
    grid_size = cos_ref.shape[2]
    part = grid_size // RADIX

    @pl.when((pl.program_id(0) == 0) & (layer == 0))
    def _():
        copy = pltpu.make_async_copy(left_ref.at[lax.axis_index("facet")], near, sem)
        copy.start()
        for p in range(RADIX):
            wide[p, :part] = fwd_ref[p]
            wide[p, part:, :part] = -fwd_ref[p][:, part:]
            wide[p, part:, part:] = fwd_ref[p][:, :part]
        copy.wait()

    @pl.when(layer == 0)
    def _():
        rows = jnp.dot(near[...], right_ref[0], preferred_element_type=jnp.float32)
        held[...] = (rows * scale_rows).astype(jnp.bfloat16)

    real = held[:band, :].astype(jnp.float32)
    imag = held[band:, :].astype(jnp.float32)
    cos = cos_ref[0]
    sin = sin_ref[0]
    s_real = (real * cos - imag * sin).astype(jnp.bfloat16)
    s_imag = (real * sin + imag * cos).astype(jnp.bfloat16)
    pieces = []
    for p in range(RADIX):
        lo, hi = p * part, (p + 1) * part
        pair = jnp.concatenate([s_real[:, lo:hi], s_imag[:, lo:hi]], 1)
        got = jnp.dot(pair, wide[p], preferred_element_type=jnp.float32)
        pieces.append((got[:, :part], got[:, part:]))
    (ar, ai), (br, bi), (cr, ci), (dr, di) = pieces
    er, ei, fr, fi = ar + cr, ai + ci, ar - cr, ai - ci
    gr, gi, hr, hi_ = br + dr, bi + di, br - dr, bi - di
    reals = jnp.concatenate([er + gr, fr + hi_, er - gr, fr - hi_], 1)
    imags = jnp.concatenate([ei + gi, fi - hr, ei - gi, fi + hr], 1)
    out_ref[0, 0, :, 0, :] = reals.astype(jnp.bfloat16)
    out_ref[0, 0, :, 1, :] = imags.astype(jnp.bfloat16)


def finish(left, right, cos, sin, forward, scale_rows):
    layers, band, grid_size = cos.shape
    slots, count, _ = right.shape
    part = grid_size // RADIX
    return pl.pallas_call(
        functools.partial(finish_kernel, band, scale_rows),
        grid=(slots, layers),
        out_shape=jax.ShapeDtypeStruct((slots, layers, band, 2, grid_size), jnp.bfloat16),
        in_specs=[
            pl.BlockSpec(memory_space=pl.ANY),
            pl.BlockSpec((1, count, grid_size), lambda s, l: (s, 0, 0)),
            pl.BlockSpec((1, band, grid_size), lambda s, l: (l, 0, 0)),
            pl.BlockSpec((1, band, grid_size), lambda s, l: (l, 0, 0)),
            pl.BlockSpec(forward.shape, lambda s, l: (0, 0, 0)),
        ],
        out_specs=pl.BlockSpec((1, 1, band, 2, grid_size), lambda s, l: (s, l, 0, 0, 0)),
        scratch_shapes=[
            pltpu.VMEM((2 * band, grid_size), jnp.bfloat16),
            pltpu.VMEM((RADIX, 2 * part, 2 * part), jnp.bfloat16),
            pltpu.VMEM((2 * band, count), jnp.bfloat16),
            pltpu.SemaphoreType.DMA,
        ],
        compiler_params=pltpu.CompilerParams(vmem_limit_bytes=48 * 1024 * 1024),
        cost_estimate=pl.CostEstimate(flops=10_000_000_000, bytes_accessed=20_000_000, transcendentals=0),
    )(left, right, cos, sin, forward)


def local(
    facet_data,
    window,
    screen_phase,
    facet_shift,
    sub_offset,
    win_start,
    win_extent,
    owner_slot,
    layer_w,
):
    facets = lax.axis_size("facet")
    owners = lax.axis_size("sub")
    teams = lax.axis_size("wa")
    strip_rows = facet_data.shape[1]
    facet_len = facet_data.shape[3]
    band, grid_size = screen_phase.shape
    part = grid_size // RADIX
    total_subs = owner_slot.shape[0]
    slots = total_subs // owners
    group = facets // slots
    chunk = strip_rows // group
    strip_total = strip_rows * owners * teams
    layers = layer_w.shape[0] // teams
    dims = (facets, owners, teams, strip_rows, facet_len, grid_size, slots, total_subs)

    outer_len = facet_len // LANES
    sig = (facet_data[0].astype(jnp.float32) * window).astype(jnp.bfloat16)
    sig = sig.reshape(strip_rows, 2 * outer_len, LANES)
    tables = strip_tables(facet_len, grid_size)
    scalars = (facet_shift, sub_offset, win_start, win_extent, owner_slot, layer_w)
    right, cos, sin = column(scalars, sig, window, tables, screen_phase, dims, layers)
    right = right.reshape(slots, 2 * strip_total, grid_size)

    g_ids, t_ids, c_ids, o_ids, r_ids = np.meshgrid(
        np.arange(group), np.arange(teams), np.arange(2), np.arange(owners), np.arange(chunk), indexing="ij"
    )
    global_row = ((o_ids * teams + t_ids) * strip_rows + g_ids * chunk + r_ids).reshape(1, 1, -1)
    is_imag = c_ids.reshape(1, 1, -1)
    my_rows = np.arange(grid_size).reshape(facets, band, 1)
    all_cos, all_sin = table(my_rows * global_row, grid_size, -1.0)
    real_rows = np.where(is_imag == 1, -all_sin, all_cos)
    imag_rows = np.where(is_imag == 1, all_cos, all_sin)
    left = jnp.asarray(np.concatenate([real_rows, imag_rows], 1).astype(jnp.bfloat16))

    v_ids = np.arange(part)[None, :] * RADIX + np.arange(RADIX)[:, None]
    fwd_cos, fwd_sin = table(v_ids[:, :, None] * np.arange(part)[None, None, :], grid_size, -1.0)
    rounded = lambda x: x.astype(jnp.bfloat16).astype(np.float64)
    forward = np.concatenate([rounded(fwd_cos), rounded(fwd_sin)], 2) / math.sqrt(grid_size)
    return finish(left, right, cos, sin, jnp.asarray(forward.astype(jnp.bfloat16)), 1.0 / math.sqrt(strip_total))


def solution(mesh):
    in_specs = (
        P("facet", ("sub", "wa"), None, None),
        P(),
        P("facet", None),
        P(),
        P(),
        P(),
        P(),
        P(),
        P(),
    )
    out_specs = P("sub", "wa", "facet", None, None)
    return jax.shard_map(local, mesh=mesh, in_specs=in_specs, out_specs=out_specs, check_vma=False)
```

time: 105 us -> 55.3 us (0.53)
  Pallas kernels: 15.3 us -> 52.4 us
  waiting for transfers between devices: 24 us -> 0 us
  other arithmetic: 16.1 us -> 0.12 us
  between operations: 15.4 us -> 0.19 us
  starting transfers between devices: 11.2 us -> 0 us
  local copies, waits for them, and re-layouts: 12.3 us -> 2.35 us
  matrix products: 9.36 us -> 0 us
    pallas_call x1 -> x2, Pallas kernels: 15.3 us -> 52.4 us  [the longest x1 36.4 us: column(): pl.pallas_call(functools.partial(column_kernel, dims), out_shape=[jax.Sha...]
    ppermute x4 -> x0, waiting for transfers between devices: 15.8 us -> none  [doubled(): other = lax.ppermute(block, axis, [(i, i ^ step) for i in range(size)])]
    dot_general x4 -> x0, matrix products: 9.36 us -> none  [the longest x1 3.87 us: local(): jnp.dot(received.reshape(facets * owners * slots * share, 2 * width), jnp...]
    sin x1 -> x0, other arithmetic: 8.62 us -> none  [local(): sin = jnp.sin(angles)]
    all_to_all x1 -> x0, waiting for transfers between devices: 8.24 us -> none  [local(): lax.all_to_all(sendable, ('facet', 'sub'), split_axis=0, concat_axis=0, t...]
    all_to_all x1 -> x0, starting transfers between devices: 7.32 us -> none  [local(): lax.all_to_all(sendable, ('facet', 'sub'), split_axis=0, concat_axis=0, t...]
    ppermute x4 -> x0, starting transfers between devices: 3.88 us -> none  [doubled(): other = lax.ppermute(block, axis, [(i, i ^ step) for i in range(size)])]
    reshape x3 -> x0, local copies, waits for them, and re-layouts: 2.9 us -> none  [the longest x1 2.02 us: facet_spectrum(): return out.reshape(strip_rows, 2, facet_len)]
  transfers between devices with their start and end apart: 5 -> 0, of which waited for: 5 -> 0; matrix products, arithmetic and copies ran while one was open for 13% -> 0% of each run, Pallas kernels for 0% -> 0%
where the time goes in v1:
time: 55.3 us; the launch traced here: 55.1 us
  Pallas kernels  52.4 us (95%)
  local copies, waits for them, and re-layouts  2.35 us (4%)
    pallas_call x1, Pallas kernels, column(): pl.pallas_call(functools.partial(column_kernel, dims), out_shape=[jax.Sha...  36.4 us
    pallas_call x1, Pallas kernels, finish(): pl.pallas_call(functools.partial(finish_kernel, band, scale_rows), grid=(...  16 us
    convert_element_type x1, local copies, waits for them, and re-layouts, local(): sig = (facet_data[0].astype(jnp.float32) * window).astype(jnp.bfloat16)  1.38 us

profile of v1, /device:TPU:0, one launch (start us, length us, event | category | flops | bytes accessed | tf_op | source)
XLA Modules:
  0.0 55.1 jit_solution(13121392174949205463)
XLA Ops:
  0.0 0.0 copy-start.5
  0.0 0.0 copy-start.2
  0.0 0.0 copy-start.1
  0.0 0.0 copy-start.4
  0.1 0.0 copy-start.3
  0.1 0.0 copy-start
  0.1 0.9 %mul.16 = f32[2,64,128]{2,1,0:T(8,128)S(1)} broadcast(f32[64,128]{1,0:T(8,128)} %bitcast.5), dimensions={1,2} | broadcast | bytes 98304 | tf_op jit(solution)/shard_map/mul | solution.py:574
  1.0 1.4 %reshape.13 = f32[16,128,128]{2,1,0:T(8,128)S(1)} reshape(bf16[1,16,2,8192]{3,2,1,0:T(2,128)(2,1)} %param.15) | data formatting | bytes 1572864 | tf_op jit(solution)/shard_map/convert_element_type | solution.py:574
  2.4 0.1 multiply_convert_fusion.sig_ref
  2.5 0.0 copy-done.7
  2.5 0.0 copy-done.10
  2.5 0.0 copy-done.11
  2.5 0.0 copy-done.12
  2.5 0.0 copy-done.6
  2.5 0.0 copy-done.5
  2.6 0.0 copy-done.2
  2.6 0.0 copy-done.1
  2.6 0.0 copy-done.4
  2.6 0.0 copy-start.8
  2.6 0.0 copy-start.9
  2.6 36.4 %shard_map.145 = (bf16[4,4,2,32,1024]{4,3,2,1,0:T(8,128)(2,1)S(1)}, f32[2,256,1024]{2,1,0:T(8,128)}, f32[2,256,1024]{2,1,0:T(8,128)}) custom-call(s32[4]{0:T(128)S(1)} %copy-done.3, s32[8]{0:T(128)S(1)} %copy-done.4, s32[4,8]{1,0:T(4,128)S(1)} %copy-done.1, s32[4,8]{1,0:T(4,128)S(1)} %copy-done.2, s32[8]{0:T(128)S(1)} %copy-done.5, s32[8]{0:T(128)S(1)} %copy-done.6, ...), custom_call_target="tpu_custom_call" | custom-call | flops 2000000000 | bytes 20000000 | tf_op jit(solution)/shard_map/pallas_call | solution.py:451
  39.1 0.0 copy-done.8
  39.1 0.0 copy-done.9
  39.1 16.0 %shard_map.146 = bf16[4,2,256,2,1024]{4,3,2,1,0:T(2,128)(2,1)} custom-call(bf16[4,512,256]{2,1,0:T(8,128)(2,1)S(1)} %copy-done.9, bf16[4,256,1024]{2,1,0:T(8,128)(2,1)S(1)} %bitcast.3, f32[2,256,1024]{2,1,0:T(8,128)} %get-tuple-element.9.cos_ref, f32[2,256,1024]{2,1,0:T(8,128)} %get-tuple-element.10.sin_ref, bf16[4,256,512]{2,1,0:T(8,128)(2,1)S(1)} %copy-done.8), custom_call_target="tpu_custom_call" | custom-call | flops 10000000000 | bytes 20000000 | tf_op jit(solution)/shard_map/pallas_call | solution.py:524
  (7 shorter events, 0.0 us)
Async XLA Ops:
  0.0 2.5 %copy-start.7 = (bf16[4,256,512]{2,1,0:T(8,128)(2,1)S(1)}, bf16[4,256,512]{2,1,0:T(8,128)(2,1)}, u32[]{:S(2)}) copy-start(bf16[4,256,512]{2,1,0:T(8,128)(2,1)} %constant.15.clone.back_ref) | copy-start | bytes 3145732
  0.0 2.5 %copy-start.10 = (bf16[256,256]{1,0:T(8,128)(2,1)S(1)}, bf16[256,256]{1,0:T(8,128)(2,1)}, u32[]{:S(2)}) copy-start(bf16[256,256]{1,0:T(8,128)(2,1)} %constant.14.clone.second_ref) | copy-start | bytes 393220
  0.0 2.5 %copy-start.11 = (f32[2,64,128]{2,1,0:T(8,128)S(1)}, f32[2,64,128]{2,1,0:T(8,128)}, u32[]{:S(2)}) copy-start(f32[2,64,128]{2,1,0:T(8,128)} %constant.13.clone.twiddle_ref) | copy-start | bytes 196612
  0.0 2.5 %copy-start.12 = (bf16[128,128]{1,0:T(8,128)(2,1)S(1)}, bf16[128,128]{1,0:T(8,128)(2,1)}, u32[]{:S(2)}) copy-start(bf16[128,128]{1,0:T(8,128)(2,1)} %constant.12.clone.first_ref) | copy-start | bytes 98308
  0.0 2.5 %copy-start.6 = (s32[8]{0:T(128)S(1)}, s32[8]{0:T(128)}, u32[]{:S(2)}) copy-start(s32[8]{0:T(128)} %level_ref.1) | copy-start | bytes 100
  0.0 2.5 %copy-start.5 = (s32[8]{0:T(128)S(1)}, s32[8]{0:T(128)}, u32[]{:S(2)}) copy-start(s32[8]{0:T(128)} %slot_ref.1) | copy-start | bytes 100
  0.0 2.5 %copy-start.2 = (s32[4,8]{1,0:T(4,128)S(1)}, s32[4,8]{1,0:T(4,128)}, u32[]{:S(2)}) copy-start(s32[4,8]{1,0:T(4,128)} %extent_ref.1) | copy-start | bytes 388
  0.0 2.5 %copy-start.1 = (s32[4,8]{1,0:T(4,128)S(1)}, s32[4,8]{1,0:T(4,128)}, u32[]{:S(2)}) copy-start(s32[4,8]{1,0:T(4,128)} %start_ref.1) | copy-start | bytes 388
  0.0 2.5 %copy-start.4 = (s32[8]{0:T(128)S(1)}, s32[8]{0:T(128)}, u32[]{:S(2)}) copy-start(s32[8]{0:T(128)} %offset_ref.1) | copy-start | bytes 100
  0.1 2.5 %copy-start.3 = (s32[4]{0:T(128)S(1)}, s32[4]{0:T(128)}, u32[]{:S(2)}) copy-start(s32[4]{0:T(128)} %shift_ref.1) | copy-start | bytes 52
  0.1 2.5 %copy-start = (f32[256,1024]{1,0:T(8,128)S(1)}, f32[256,1024]{1,0:T(8,128)}, u32[]{:S(2)}) copy-start(f32[256,1024]{1,0:T(8,128)} %phase_ref.1) | copy-start | bytes 3145732
  2.6 36.5 %copy-start.8 = (bf16[4,256,512]{2,1,0:T(8,128)(2,1)S(1)}, bf16[4,256,512]{2,1,0:T(8,128)(2,1)}, u32[]{:S(2)}) copy-start(bf16[4,256,512]{2,1,0:T(8,128)(2,1)} %constant.17.clone.fwd_ref) | copy-start | bytes 3145732
  2.6 36.5 %copy-start.9 = (bf16[4,512,256]{2,1,0:T(8,128)(2,1)S(1)}, bf16[4,512,256]{2,1,0:T(8,128)(2,1)}, u32[]{:S(2)}) copy-start(bf16[4,512,256]{2,1,0:T(8,128)(2,1)} %constant.16.clone.left_ref) | copy-start | bytes 3145732

commit v2 on v1

--- a/solution.py
+++ b/solution.py
@@ -11,7 +11,10 @@
 
 RADIX = 4
 LANES = 128
-PARTS = 2
+PARTS = 4
+HALVES = 2
+VMEM_COLUMN = 32 * 1024 * 1024
+VMEM_FINISH = 32 * 1024 * 1024
 MESH = pl.DeviceIdType.MESH
 
 
@@ -62,6 +65,61 @@
     return first, twiddle, second, back
 
 
+def arrivals(facets, facet_id):
+    order = []
+    for z in range(facets):
+        row = [z]
+        for d in range(1, facets):
+            row += [f for f in (z - d, z + d) if 0 <= f < facets]
+        order.append(row)
+    picked = []
+    for k in range(facets):
+        value = 0
+        for z in range(facets):
+            gap = facet_id - z
+            here = 1 - lax.div(gap * gap + (facets * facets - 1), facets * facets)
+            value = value + here * order[z][k]
+        picked.append(value)
+    return picked
+
+
+def unit(step, right_ref, slot, near_ref, fwd_ref, cos_ref, sin_ref, held, out_ref):
+    layers, band, grid_size = cos_ref.shape
+    part = grid_size // RADIX
+    half = band // HALVES
+    layer = lax.rem(step, layers)
+    which = lax.div(step, layers)
+    rows = pl.ds(pl.multiple_of(which * half, half), half)
+
+    @pl.when(layer == 0)
+    def _():
+        right = right_ref[slot].reshape(near_ref.shape[2], grid_size)
+        for p in range(RADIX):
+            lanes = slice(p * part, (p + 1) * part)
+            got = jnp.dot(near_ref[which], right[:, lanes], preferred_element_type=jnp.float32)
+            held[:, lanes] = got.astype(jnp.bfloat16)
+
+    pieces = []
+    for p in range(RADIX):
+        lanes = slice(p * part, (p + 1) * part)
+        real = held[:half, lanes].astype(jnp.float32)
+        imag = held[half:, lanes].astype(jnp.float32)
+        cos = cos_ref[layer, rows, lanes]
+        sin = sin_ref[layer, rows, lanes]
+        s_real = (real * cos - imag * sin).astype(jnp.bfloat16)
+        s_imag = (real * sin + imag * cos).astype(jnp.bfloat16)
+        pair = jnp.concatenate([s_real, s_imag], 1)
+        got = jnp.dot(pair, fwd_ref[p], preferred_element_type=jnp.float32)
+        pieces.append((got[:, :part], got[:, part:]))
+    (ar, ai), (br, bi), (cr, ci), (dr, di) = pieces
+    er, ei, fr, fi = ar + cr, ai + ci, ar - cr, ai - ci
+    gr, gi, hr, hi_ = br + dr, bi + di, br - dr, bi - di
+    reals = jnp.concatenate([er + gr, fr + hi_, er - gr, fr - hi_], 1)
+    imags = jnp.concatenate([ei + gi, fi - hr, ei - gi, fi + hr], 1)
+    out_ref[layer, rows, 0, :] = reals.astype(jnp.bfloat16)
+    out_ref[layer, rows, 1, :] = imags.astype(jnp.bfloat16)
+
+
 def column_kernel(
     dims,
     shift_ref,
@@ -76,19 +134,25 @@
     second_ref,
     back_ref,
     phase_ref,
+    left_ref,
     gather_ref,
     cos_ref,
     sin_ref,
+    near_ref,
+    fwd_ref,
+    done_ref,
     mid,
     spec,
     turn,
     outgoing,
     incoming,
     wide,
+    held,
     pack_send,
     pack_recv,
     plane_send,
     block_recv,
+    near_sem,
 ):
     facets, owners, teams, strip_rows, facet_len, grid_size, slots, total_subs = dims
     facet_id = lax.axis_index("facet")
@@ -126,6 +190,9 @@
     pl.semaphore_signal(barrier, inc=1, device_id=(facet_id, sub_id, sibling), device_id_type=MESH)
     peers += 1
 
+    near_copy = pltpu.make_async_copy(left_ref.at[facet_id], near_ref, near_sem)
+    near_copy.start()
+
     def holder(slot):
         def look(j, found):
             return jnp.where(slot_ref[j] == slot, j, found)
@@ -165,14 +232,14 @@
 
     lax.fori_loop(0, strip_rows // fold, second_step, 0)
 
-    held = [holder(p) for p in range(total_subs)]
+    holders = [holder(p) for p in range(total_subs)]
     row_ids = lax.broadcasted_iota(jnp.int32, (total_subs, width), 0)
     k_ids = lax.broadcasted_iota(jnp.int32, (total_subs, width), 1)
     starts = jnp.zeros((total_subs, width), jnp.int32)
     extents = jnp.zeros((total_subs, width), jnp.int32)
     for p in range(total_subs):
-        starts = jnp.where(row_ids == p, start_ref[facet_id, held[p]], starts)
-        extents = jnp.where(row_ids == p, extent_ref[facet_id, held[p]], extents)
+        starts = jnp.where(row_ids == p, start_ref[facet_id, holders[p]], starts)
+        extents = jnp.where(row_ids == p, extent_ref[facet_id, holders[p]], extents)
     product = (shift_ref[facet_id] * (starts + k_ids)) & (grid_size - 1)
     turn_cos, turn_sin = sincos(product.astype(jnp.float32) * (2.0 * math.pi / grid_size))
     inside = k_ids < extents
@@ -251,6 +318,7 @@
         wide[p, :part] = back_ref[p]
         wide[p, part:, :part] = -back_ref[p][:, part:]
         wide[p, part:, part:] = back_ref[p][:, :part]
+        fwd_ref[p] = wide[p].T
     mine = holder(sub_id * slots + my_slot)
     f_rows = lax.broadcasted_iota(jnp.int32, (facets, grid_size), 0)
     at = lax.broadcasted_iota(jnp.int32, (facets, grid_size), 1)
@@ -261,7 +329,8 @@
     ramp_cos, ramp_sin = sincos(
         ((begins * v_ids) & (grid_size - 1)).astype(jnp.float32) * (2.0 * math.pi / grid_size)
     )
-    scale_col = 1.0 / math.sqrt(facets * grid_size)
+    strip_total = strip_rows * owners * teams
+    scale_col = 1.0 / math.sqrt(facets * grid_size) / math.sqrt(strip_total) / math.sqrt(grid_size)
     ramp_cos = ramp_cos * scale_col
     ramp_sin = ramp_sin * scale_col
 
@@ -324,8 +393,11 @@
             total_i = total_i + (real * sin + imag * cos)
         images[0].append(total_r)
         images[1].append(total_i)
-    for c in range(2):
-        gather_ref[facet_id, team_id, c] = jnp.concatenate(images[c], 1).astype(jnp.bfloat16)
+    piece_rows = 2 * rows_f // PARTS
+    image = jnp.concatenate([jnp.concatenate(images[c], 1) for c in range(2)], 0).astype(jnp.bfloat16)
+    for h in range(PARTS):
+        gather_ref[facet_id, team_id, h] = image[h * piece_rows : (h + 1) * piece_rows]
+    near_copy.wait()
 
     def send(kind, f, team, h, target):
         return pltpu.make_async_remote_copy(
@@ -337,98 +409,137 @@
             device_id_type=MESH,
         )
 
+    def start(copy):
+        copy.start()
+
+    def finish_send(copy):
+        copy.wait_send()
+
     def arrive(f, team, h):
         send(0, f, team, h, (facet_id, sub_id, team_id)).wait_recv()
 
-    has_next = facet_id < facets - 1
-    has_last = facet_id > 0
     below = jnp.maximum(facet_id - 1, 0)
     above = jnp.minimum(facet_id + 1, facets - 1)
 
-    def along(f, h, up, act):
-        if up is None or up:
-
-            @pl.when(has_next)
-            def _():
-                act(send(0, f, team_id, h, (above, sub_id, team_id)))
-
-        if up is None or not up:
-
-            @pl.when(has_last)
-            def _():
-                act(send(0 if up is not None else 1, f, team_id, h, (below, sub_id, team_id)))
-
+    def upward(f, h, act):
+        @pl.when(facet_id < facets - 1)
+        def _():
+            act(send(0, f, team_id, h, (above, sub_id, team_id)))
+
+    def downward(f, h, act):
+        @pl.when(facet_id > 0)
+        def _():
+            act(send(1, f, team_id, h, (below, sub_id, team_id)))
+
+    def across(f, h, act):
         for step in range(1, spread):
             act(send(1 + step, f, team_id, h, (facet_id, sub_id, team_at(step))))
-        act(send(1 + spread, f, team_id, h, (facet_id, sub_id, sibling)))
 
     def aside(f, team, h, act):
         act(send(1 + spread, f, team, h, (facet_id, sub_id, sibling)))
 
-    def start(copy):
-        copy.start()
-
-    def finish_send(copy):
-        copy.wait_send()
-
-    def guarded(condition, body):
-        if condition is None:
-            body()
-        else:
-            pl.when(condition)(body)
-
-    def sides(d):
-        yield True, facet_id >= d, jnp.maximum(facet_id - d, 0)
-        yield False, facet_id < facets - d, jnp.minimum(facet_id + d, facets - 1)
-
-    def partners(d, h):
+    def from_below(d, h):
+        @pl.when(facet_id >= d)
+        def _():
+            f = jnp.maximum(facet_id - d, 0)
+            arrive(f, team_id, h)
+            upward(f, h, start)
+            across(f, h, start)
+            aside(f, team_id, h, start)
+
+    def from_above(d, h):
+        @pl.when(facet_id < facets - d)
+        def _():
+            f = jnp.minimum(facet_id + d, facets - 1)
+            arrive(f, team_id, h)
+            downward(f, h, start)
+            aside(f, team_id, h, start)
+            if d > 1:
+                across(f, h, start)
+            else:
+                pl.when(facet_id == 0)(lambda: across(f, h, start))
+
+    def late_across(h):
+        @pl.when((facet_id > 0) & (facet_id < facets - 1))
+        def _():
+            across(above, h, start)
+
+    def partner(f, h):
         for step in range(1, spread):
-            if d == 0:
-                arrive(facet_id, team_at(step), h)
-                aside(facet_id, team_at(step), h, start)
-            else:
-                for _, condition, f in sides(d):
-
-                    def body(f=f, step=step):
-                        arrive(f, team_at(step), h)
-                        aside(f, team_at(step), h, start)
-
-                    pl.when(condition)(body)
-
-    for h in range(PARTS):
-        along(facet_id, h, None, start)
-    for d in range(1, facets):
-        for h in range(PARTS):
-            for up, condition, f in sides(d):
-
-                def body(f=f, h=h, up=up):
-                    arrive(f, team_id, h)
-                    along(f, h, up, start)
-
-                pl.when(condition)(body)
-            partners(d - 1, h)
-    for h in range(PARTS):
-        partners(facets - 1, h)
-    for off in range(facets):
-        for h in range(PARTS):
-            f = lax.rem(facet_id + off, facets)
-            for step in range(spread):
-                arrive(f, lax.rem(sibling + cores * step, teams), h)
-
-    for h in range(PARTS):
-        along(facet_id, h, None, finish_send)
+            arrive(f, team_at(step), h)
+            aside(f, team_at(step), h, start)
+
+    def settled(f, h):
+        for step in range(spread):
+            arrive(f, lax.rem(sibling + cores * step, teams), h)
+
+    def each_part(body):
+        def run(h, carry):
+            body(h)
+            return carry
+
+        lax.fori_loop(0, PARTS, run, 0)
+
+    sequence = arrivals(facets, facet_id)
+    early = facets - 1 if done_ref.shape[2] == cos_ref.shape[1] else 0
+
+    def own(h):
+        upward(facet_id, h, start)
+        downward(facet_id, h, start)
+        across(facet_id, h, start)
+        aside(facet_id, team_id, h, start)
+
+    each_part(own)
+
+    def neighbours(h):
+        from_below(1, h)
+        from_above(1, h)
+        partner(facet_id, h)
+
+    each_part(neighbours)
+    each_part(late_across)
+    each_part(lambda h: settled(sequence[0], h))
+    for k in range(facets - 1):
+
+        def relay(h, k=k):
+            if k + 2 < facets:
+                from_below(k + 2, h)
+                from_above(k + 2, h)
+            partner(sequence[k + 1], h)
+            if k < early:
+                unit(h, gather_ref, sequence[k], near_ref, fwd_ref, cos_ref, sin_ref, held, done_ref.at[k])
+
+        each_part(relay)
+        each_part(lambda h, k=k: settled(sequence[k + 1], h))
+
+    def drain(h):
+        upward(facet_id, h, finish_send)
+        downward(facet_id, h, finish_send)
+        across(facet_id, h, finish_send)
+        aside(facet_id, team_id, h, finish_send)
         for step in range(1, spread):
             aside(facet_id, team_at(step), h, finish_send)
-    for d in range(1, facets):
-        for h in range(PARTS):
-            for up, condition, f in sides(d):
-
-                def body(f=f, h=h, up=up):
-                    along(f, h, up, finish_send)
-                    for step in range(1, spread):
-                        aside(f, team_at(step), h, finish_send)
-
-                pl.when(condition)(body)
+        for d in range(1, facets):
+
+            @pl.when(facet_id >= d)
+            def _(d=d):
+                f = jnp.maximum(facet_id - d, 0)
+                upward(f, h, finish_send)
+                across(f, h, finish_send)
+                aside(f, team_id, h, finish_send)
+                for step in range(1, spread):
+                    aside(f, team_at(step), h, finish_send)
+
+            @pl.when(facet_id < facets - d)
+            def _(d=d):
+                f = jnp.minimum(facet_id + d, facets - 1)
+                downward(f, h, finish_send)
+                across(f, h, finish_send)
+                aside(f, team_id, h, finish_send)
+                for step in range(1, spread):
+                    aside(f, team_at(step), h, finish_send)
+
+    each_part(drain)
     for copy, away in packs:
         if away is True:
             copy.wait_send()
@@ -436,7 +547,7 @@
             pl.when(away)(copy.wait_send)
 
 
-def column(scalars, sig, window_rows, tables, phase, dims, layers):
+def column(scalars, sig, tables, left, phase, dims, layers, early):
     facets, owners, teams, strip_rows, facet_len, grid_size, slots, total_subs = dims
     first, twiddle, second, back = [jnp.asarray(x) for x in tables]
     group = facets // slots
@@ -446,7 +557,7 @@
     band = phase.shape[0]
     smem = pl.BlockSpec(memory_space=pltpu.SMEM)
     vmem = pl.BlockSpec(memory_space=pltpu.VMEM)
-    blocks = (facets, teams, 2, owners * chunk, grid_size)
+    blocks = (facets, teams, PARTS, 2 * owners * chunk // PARTS, grid_size)
     spread = teams // 2
     return pl.pallas_call(
         functools.partial(column_kernel, dims),
@@ -454,9 +565,12 @@
             jax.ShapeDtypeStruct(blocks, jnp.bfloat16),
             jax.ShapeDtypeStruct((layers, band, grid_size), jnp.float32),
             jax.ShapeDtypeStruct((layers, band, grid_size), jnp.float32),
+            jax.ShapeDtypeStruct(left.shape[1:], jnp.bfloat16),
+            jax.ShapeDtypeStruct((RADIX, 2 * part, 2 * part), jnp.bfloat16),
+            jax.ShapeDtypeStruct((max(early, 1), layers, band if early else 16, 2, grid_size), jnp.bfloat16),
         ],
-        in_specs=[smem] * 6 + [vmem] * 6,
-        out_specs=[vmem] * 3,
+        in_specs=[smem] * 6 + [vmem] * 6 + [pl.BlockSpec(memory_space=pl.ANY)],
+        out_specs=[vmem] * 6,
         scratch_shapes=[
             pltpu.VMEM((strip_rows * (facet_len // LANES), 2 * LANES), jnp.bfloat16),
             pltpu.VMEM((2 * facet_len // LANES, strip_rows, LANES), jnp.float32),
@@ -464,84 +578,74 @@
             pltpu.VMEM((facets * owners, chunk, 2 * width), jnp.bfloat16),
             pltpu.VMEM((facets, owners, chunk, 2 * width), jnp.bfloat16),
             pltpu.VMEM((RADIX, 2 * part, 2 * part), jnp.bfloat16),
+            pltpu.VMEM((2 * band // HALVES, grid_size), jnp.bfloat16),
             pltpu.SemaphoreType.DMA((facets * owners,)),
             pltpu.SemaphoreType.DMA((facets, owners)),
             pltpu.SemaphoreType.DMA((2 + spread, facets, spread, PARTS)),
             pltpu.SemaphoreType.DMA((facets, teams, PARTS)),
+            pltpu.SemaphoreType.DMA,
         ],
         compiler_params=pltpu.CompilerParams(
-            collective_id=0, has_side_effects=True, vmem_limit_bytes=48 * 1024 * 1024
+            collective_id=0, has_side_effects=True, vmem_limit_bytes=VMEM_COLUMN
         ),
         cost_estimate=pl.CostEstimate(flops=2_000_000_000, bytes_accessed=20_000_000, transcendentals=0),
-    )(*scalars, sig, first, twiddle, second, back, phase)
-
-
-def finish_kernel(band, scale_rows, left_ref, right_ref, cos_ref, sin_ref, fwd_ref, out_ref, held, wide, near, sem):
-    layer = pl.program_id(1)
-    grid_size = cos_ref.shape[2]
-    part = grid_size // RADIX
-
-    @pl.when((pl.program_id(0) == 0) & (layer == 0))
-    def _():
-        copy = pltpu.make_async_copy(left_ref.at[lax.axis_index("facet")], near, sem)
-        copy.start()
-        for p in range(RADIX):
-            wide[p, :part] = fwd_ref[p]
-            wide[p, part:, :part] = -fwd_ref[p][:, part:]
-            wide[p, part:, part:] = fwd_ref[p][:, :part]
+    )(*scalars, sig, first, twiddle, second, back, phase, left)
+
+
+def finish_kernel(early, facets, right_ref, cos_ref, sin_ref, near_ref, fwd_ref, done_ref, out_ref, held, ready, done_sem, ready_sem):
+    layers, band, grid_size = cos_ref.shape
+    slots = out_ref.shape[0]
+    half = band // HALVES
+    if early:
+        sequence = arrivals(facets, lax.axis_index("facet"))
+    else:
+        sequence = list(range(slots))
+    moved = []
+    for k in range(early):
+        moved.append(pltpu.make_async_copy(done_ref.at[k], out_ref.at[sequence[k]], done_sem.at[k]))
+        moved[-1].start()
+
+    def ship(slot, step):
+        layer = lax.rem(step, layers)
+        rows = pl.ds(pl.multiple_of(lax.div(step, layers) * half, half), half)
+        return pltpu.make_async_copy(
+            ready.at[layer, rows], out_ref.at[slot, layer, rows], ready_sem.at[step]
+        )
+
+    for k in range(early, slots):
+
+        def run(step, carry, k=k):
+            if k > early:
+                ship(sequence[k - 1], step).wait()
+            unit(step, right_ref, sequence[k], near_ref, fwd_ref, cos_ref, sin_ref, held, ready)
+            ship(sequence[k], step).start()
+            return carry
+
+        lax.fori_loop(0, layers * HALVES, run, 0)
+    for step in range(layers * HALVES):
+        ship(sequence[slots - 1], step).wait()
+    for copy in moved:
         copy.wait()
 
-    @pl.when(layer == 0)
-    def _():
-        rows = jnp.dot(near[...], right_ref[0], preferred_element_type=jnp.float32)
-        held[...] = (rows * scale_rows).astype(jnp.bfloat16)
-
-    real = held[:band, :].astype(jnp.float32)
-    imag = held[band:, :].astype(jnp.float32)
-    cos = cos_ref[0]
-    sin = sin_ref[0]
-    s_real = (real * cos - imag * sin).astype(jnp.bfloat16)
-    s_imag = (real * sin + imag * cos).astype(jnp.bfloat16)
-    pieces = []
-    for p in range(RADIX):
-        lo, hi = p * part, (p + 1) * part
-        pair = jnp.concatenate([s_real[:, lo:hi], s_imag[:, lo:hi]], 1)
-        got = jnp.dot(pair, wide[p], preferred_element_type=jnp.float32)
-        pieces.append((got[:, :part], got[:, part:]))
-    (ar, ai), (br, bi), (cr, ci), (dr, di) = pieces
-    er, ei, fr, fi = ar + cr, ai + ci, ar - cr, ai - ci
-    gr, gi, hr, hi_ = br + dr, bi + di, br - dr, bi - di
-    reals = jnp.concatenate([er + gr, fr + hi_, er - gr, fr - hi_], 1)
-    imags = jnp.concatenate([ei + gi, fi - hr, ei - gi, fi + hr], 1)
-    out_ref[0, 0, :, 0, :] = reals.astype(jnp.bfloat16)
-    out_ref[0, 0, :, 1, :] = imags.astype(jnp.bfloat16)
-
-
-def finish(left, right, cos, sin, forward, scale_rows):
+
+def finish(right, cos, sin, near, fwd, done, early, facets):
     layers, band, grid_size = cos.shape
-    slots, count, _ = right.shape
-    part = grid_size // RADIX
+    slots = right.shape[0]
+    vmem = pl.BlockSpec(memory_space=pltpu.VMEM)
     return pl.pallas_call(
-        functools.partial(finish_kernel, band, scale_rows),
-        grid=(slots, layers),
+        functools.partial(finish_kernel, early, facets),
         out_shape=jax.ShapeDtypeStruct((slots, layers, band, 2, grid_size), jnp.bfloat16),
-        in_specs=[
-            pl.BlockSpec(memory_space=pl.ANY),
-            pl.BlockSpec((1, count, grid_size), lambda s, l: (s, 0, 0)),
-            pl.BlockSpec((1, band, grid_size), lambda s, l: (l, 0, 0)),
-            pl.BlockSpec((1, band, grid_size), lambda s, l: (l, 0, 0)),
-            pl.BlockSpec(forward.shape, lambda s, l: (0, 0, 0)),
+        in_specs=[vmem] * 6,
+        out_specs=pl.BlockSpec(memory_space=pl.ANY),
+        scratch_shapes=[
+            pltpu.VMEM((2 * band // HALVES, grid_size), jnp.bfloat16),
+            pltpu.VMEM((layers, band, 2, grid_size), jnp.bfloat16),
+            pltpu.SemaphoreType.DMA((max(early, 1),)),
+            pltpu.SemaphoreType.DMA((layers * HALVES,)),
         ],
-        out_specs=pl.BlockSpec((1, 1, band, 2, grid_size), lambda s, l: (s, l, 0, 0, 0)),
-        scratch_shapes=[
-            pltpu.VMEM((2 * band, grid_size), jnp.bfloat16),
-            pltpu.VMEM((RADIX, 2 * part, 2 * part), jnp.bfloat16),
-            pltpu.VMEM((2 * band, count), jnp.bfloat16),
-            pltpu.SemaphoreType.DMA,
-        ],
-        compiler_params=pltpu.CompilerParams(vmem_limit_bytes=48 * 1024 * 1024),
-        cost_estimate=pl.CostEstimate(flops=10_000_000_000, bytes_accessed=20_000_000, transcendentals=0),
-    )(left, right, cos, sin, forward)
+        compiler_params=pltpu.CompilerParams(vmem_limit_bytes=VMEM_FINISH),
+        cost_estimate=pl.CostEstimate(flops=2_000_000_000, bytes_accessed=20_000_000, transcendentals=0),
+    )(right, cos, sin, near, fwd, done)
 
 
 def local(
@@ -561,7 +665,6 @@
     strip_rows = facet_data.shape[1]
     facet_len = facet_data.shape[3]
     band, grid_size = screen_phase.shape
-    part = grid_size // RADIX
     total_subs = owner_slot.shape[0]
     slots = total_subs // owners
     group = facets // slots
@@ -575,25 +678,23 @@
     sig = sig.reshape(strip_rows, 2 * outer_len, LANES)
     tables = strip_tables(facet_len, grid_size)
     scalars = (facet_shift, sub_offset, win_start, win_extent, owner_slot, layer_w)
-    right, cos, sin = column(scalars, sig, window, tables, screen_phase, dims, layers)
-    right = right.reshape(slots, 2 * strip_total, grid_size)
-
     g_ids, t_ids, c_ids, o_ids, r_ids = np.meshgrid(
         np.arange(group), np.arange(teams), np.arange(2), np.arange(owners), np.arange(chunk), indexing="ij"
     )
     global_row = ((o_ids * teams + t_ids) * strip_rows + g_ids * chunk + r_ids).reshape(1, 1, -1)
     is_imag = c_ids.reshape(1, 1, -1)
-    my_rows = np.arange(grid_size).reshape(facets, band, 1)
+    my_rows = np.arange(grid_size).reshape(facets * HALVES, band // HALVES, 1)
     all_cos, all_sin = table(my_rows * global_row, grid_size, -1.0)
     real_rows = np.where(is_imag == 1, -all_sin, all_cos)
     imag_rows = np.where(is_imag == 1, all_cos, all_sin)
-    left = jnp.asarray(np.concatenate([real_rows, imag_rows], 1).astype(jnp.bfloat16))
-
-    v_ids = np.arange(part)[None, :] * RADIX + np.arange(RADIX)[:, None]
-    fwd_cos, fwd_sin = table(v_ids[:, :, None] * np.arange(part)[None, None, :], grid_size, -1.0)
-    rounded = lambda x: x.astype(jnp.bfloat16).astype(np.float64)
-    forward = np.concatenate([rounded(fwd_cos), rounded(fwd_sin)], 2) / math.sqrt(grid_size)
-    return finish(left, right, cos, sin, jnp.asarray(forward.astype(jnp.bfloat16)), 1.0 / math.sqrt(strip_total))
+    left = np.concatenate([real_rows, imag_rows], 1).astype(jnp.bfloat16)
+    left = jnp.asarray(left.reshape(facets, HALVES, 2 * band // HALVES, 2 * strip_total))
+
+    early = facets - 1 if group == 1 and layers * HALVES == PARTS else 0
+    right, cos, sin, near, fwd, done = column(scalars, sig, tables, left, screen_phase, dims, layers, early)
+    if not early:
+        right = right.reshape(slots, 2 * strip_total, grid_size)
+    return finish(right, cos, sin, near, fwd, done, early, facets)
 
 
 def solution(mesh):

time: 55.3 us -> 46.7 us (0.84)
  Pallas kernels: 52.4 us -> 40.7 us
  local copies, waits for them, and re-layouts: 2.35 us -> 4.24 us
  other arithmetic: 0.12 us -> 1.34 us
    pallas_call x1, Pallas kernels: 16 us -> 4.17 us  [finish(): pl.pallas_call(functools.partial(finish_kernel, early, facets), out_shape...]
    convert_element_type x1, other arithmetic: 0.12 us -> 1.34 us  [local(): sig = (facet_data[0].astype(jnp.float32) * window).astype(jnp.bfloat16)]
    convert_element_type x1, local copies, waits for them, and re-layouts: 1.38 us -> 2.45 us  [local(): sig = (facet_data[0].astype(jnp.float32) * window).astype(jnp.bfloat16)]
    unnamed x26 -> x24, local copies, waits for them, and re-layouts: 0.06 us -> 0.88 us
where the time goes in v2:
time: 46.7 us; the launch traced here: 46.5 us
  Pallas kernels  40.7 us (87%)
  local copies, waits for them, and re-layouts  4.24 us (9%)
  other arithmetic  1.34 us (3%)
    pallas_call x1, Pallas kernels, column(): pl.pallas_call(functools.partial(column_kernel, dims), out_shape=[jax.Sha...  36.6 us
    pallas_call x1, Pallas kernels, finish(): pl.pallas_call(functools.partial(finish_kernel, early, facets), out_shape...  4.17 us
    convert_element_type x1, local copies, waits for them, and re-layouts, local(): sig = (facet_data[0].astype(jnp.float32) * window).astype(jnp.bfloat16)  2.45 us
    convert_element_type x1, other arithmetic, local(): sig = (facet_data[0].astype(jnp.float32) * window).astype(jnp.bfloat16)  1.34 us

profile of v2, /device:TPU:0, one launch (start us, length us, event | category | flops | bytes accessed | tf_op | source)
XLA Modules:
  0.0 46.5 jit_solution(13743249146970166160)
XLA Ops:
  0.0 0.0 copy-start.5
  0.0 0.0 copy-start.2
  0.0 0.0 copy-start.1
  0.0 0.0 copy-start.4
  0.1 0.0 copy-start.3
  0.1 0.0 copy-start
  0.1 0.9 %mul.16 = f32[2,64,128]{2,1,0:T(8,128)S(1)} broadcast(f32[64,128]{1,0:T(8,128)} %bitcast.3), dimensions={1,2} | broadcast | bytes 98304 | tf_op jit(solution)/shard_map/mul | solution.py:677
  1.0 2.4 %reshape.9 = f32[16,128,128]{2,1,0:T(8,128)} reshape(bf16[1,16,2,8192]{3,2,1,0:T(2,128)(2,1)} %param.14) | data formatting | bytes 1572864 | tf_op jit(solution)/shard_map/convert_element_type | solution.py:677
  3.4 1.3 %multiply_convert_fusion.sig_ref = bf16[16,128,128]{2,1,0:T(8,128)(2,1)S(1)} fusion(f32[16,128,128]{2,1,0:T(8,128)} %reshape.9, f32[128,128]{1,0:T(8,128)S(1)} %bitcast.2), kind=kLoop, calls=%fused_computation | loop fusion | flops 524288 | bytes 1638400 | tf_op jit(solution)/shard_map/convert_element_type | solution.py:677
  4.8 0.0 copy-done.7
  4.8 0.0 copy-done.9
  4.8 0.0 copy-done.11
  4.8 0.0 copy-done.8
  4.8 0.0 copy-done.6
  4.8 0.0 copy-done.5
  4.8 0.0 copy-done.2
  4.9 0.0 copy-done.1
  4.9 0.0 copy-done.4
  4.9 0.0 copy-done.3
  4.9 0.0 copy-done
  4.9 0.0 copy-start.10
  4.9 0.8 %copy-done.10 = f32[2,64,128]{2,1,0:T(8,128)S(1)} copy-done((f32[2,64,128]{2,1,0:T(8,128)S(1)}, f32[2,64,128]{2,1,0:T(8,128)}, u32[]{:S(2)}) %copy-start.10) | copy-done | bytes 65560
  5.7 36.6 %shard_map.136 = (bf16[4,4,4,16,1024]{4,3,2,1,0:T(8,128)(2,1)S(1)}, f32[2,256,1024]{2,1,0:T(8,128)S(1)}, f32[2,256,1024]{2,1,0:T(8,128)S(1)}, bf16[2,256,256]{2,...) custom-call(s32[4]{0:T(128)S(1)} %copy-done.3, s32[8]{0:T(128)S(1)} %copy-done.4, ...), custom_call_target="tpu_custom_call" | custom-call | flops 2000000000 | bytes 20000000 | tf_op jit(solution)/shard_map/pallas_call | solution.py:562
  42.3 4.2 %shard_map.137 = bf16[4,2,256,2,1024]{4,3,2,1,0:T(2,128)(2,1)} custom-call(bf16[4,4,4,16,1024]{4,3,2,1,0:T(8,128)(2,1)S(1)} %get-tuple-element.11.right_ref, f32[2,256,1024]{2,1,0:T(8,128)S(1)} %get-tuple-element.12.cos_ref, f32[2,256,1024]{2,1,0:T(8,128)S(1)} %get-tuple-element.13.sin_ref, bf16[2,256,256]{2,1,0:T(8,128)(2,1)S(1)} %get-tuple-element.14.near_ref, ...), custom_call_target="tpu_custom_call" | custom-call | flops 2000000000 | bytes 20000000 | tf_op jit(solution)/shard_map/pallas_call | solution.py:635
  (5 shorter events, 0.0 us)
Async XLA Ops:
  0.0 4.8 %copy-start.7 = (bf16[4,256,512]{2,1,0:T(8,128)(2,1)S(1)}, bf16[4,256,512]{2,1,0:T(8,128)(2,1)}, u32[]{:S(2)}) copy-start(bf16[4,256,512]{2,1,0:T(8,128)(2,1)} %constant.14.clone.back_ref) | copy-start | bytes 3145732
  0.0 4.8 %copy-start.9 = (bf16[256,256]{1,0:T(8,128)(2,1)S(1)}, bf16[256,256]{1,0:T(8,128)(2,1)}, u32[]{:S(2)}) copy-start(bf16[256,256]{1,0:T(8,128)(2,1)} %constant.13.clone.second_ref) | copy-start | bytes 393220
  0.0 4.8 %copy-start.11 = (bf16[128,128]{1,0:T(8,128)(2,1)S(1)}, bf16[128,128]{1,0:T(8,128)(2,1)}, u32[]{:S(2)}) copy-start(bf16[128,128]{1,0:T(8,128)(2,1)} %constant.11.clone.first_ref) | copy-start | bytes 98308
  0.0 4.8 %copy-start.8 = (bf16[4,2,256,256]{3,2,1,0:T(8,128)(2,1)S(1)}, bf16[4,2,256,256]{3,2,1,0:T(8,128)(2,1)}, u32[]{:S(2)}) copy-start(bf16[4,2,256,256]{3,2,1,0:T(8,128)(2,1)} %constant.10.clone.left_ref) | copy-start | bytes 3145732
  0.0 4.8 %copy-start.6 = (s32[8]{0:T(128)S(1)}, s32[8]{0:T(128)}, u32[]{:S(2)}) copy-start(s32[8]{0:T(128)} %level_ref.1) | copy-start | bytes 100
  0.0 4.8 %copy-start.5 = (s32[8]{0:T(128)S(1)}, s32[8]{0:T(128)}, u32[]{:S(2)}) copy-start(s32[8]{0:T(128)} %slot_ref.1) | copy-start | bytes 100
  0.0 4.8 %copy-start.2 = (s32[4,8]{1,0:T(4,128)S(1)}, s32[4,8]{1,0:T(4,128)}, u32[]{:S(2)}) copy-start(s32[4,8]{1,0:T(4,128)} %extent_ref.1) | copy-start | bytes 388
  0.0 4.8 %copy-start.1 = (s32[4,8]{1,0:T(4,128)S(1)}, s32[4,8]{1,0:T(4,128)}, u32[]{:S(2)}) copy-start(s32[4,8]{1,0:T(4,128)} %start_ref.1) | copy-start | bytes 388
  0.0 4.8 %copy-start.4 = (s32[8]{0:T(128)S(1)}, s32[8]{0:T(128)}, u32[]{:S(2)}) copy-start(s32[8]{0:T(128)} %offset_ref.1) | copy-start | bytes 100
  0.1 4.8 %copy-start.3 = (s32[4]{0:T(128)S(1)}, s32[4]{0:T(128)}, u32[]{:S(2)}) copy-start(s32[4]{0:T(128)} %shift_ref.1) | copy-start | bytes 52
  0.1 4.8 %copy-start = (f32[256,1024]{1,0:T(8,128)S(1)}, f32[256,1024]{1,0:T(8,128)}, u32[]{:S(2)}) copy-start(f32[256,1024]{1,0:T(8,128)} %phase_ref.1) | copy-start | bytes 3145732
  4.9 0.8 %copy-start.10 = (f32[2,64,128]{2,1,0:T(8,128)S(1)}, f32[2,64,128]{2,1,0:T(8,128)}, u32[]{:S(2)}) copy-start(f32[2,64,128]{2,1,0:T(8,128)} %constant.12.clone.twiddle_ref) | copy-start | bytes 196612

commit v3 on v2

--- a/solution.py
+++ b/solution.py
@@ -50,7 +50,8 @@
     outer_ids = np.arange(outer_len)
     inner_ids = np.arange(inner_len)
     c1, s1 = table(outer_ids[:, None] * outer_ids[None, :], outer_len, -1.0)
-    first = np.block([[c1, -s1], [s1, c1]]).astype(jnp.bfloat16)
+    first = np.block([[c1, -s1], [s1, c1]])
+    first = first.reshape(-1, 2, outer_len).transpose(0, 2, 1).reshape(-1, 2 * outer_len).astype(jnp.bfloat16)
     ct, st = table(outer_ids[:, None] * inner_ids[None, :], facet_len, -1.0)
     twiddle = np.stack([ct, st]).astype(np.float32)
     fold = LANES // outer_len
@@ -120,40 +121,34 @@
     out_ref[layer, rows, 1, :] = imags.astype(jnp.bfloat16)
 
 
-def column_kernel(
-    dims,
-    shift_ref,
-    offset_ref,
-    start_ref,
-    extent_ref,
-    slot_ref,
-    level_ref,
-    sig_ref,
-    first_ref,
-    twiddle_ref,
-    second_ref,
-    back_ref,
-    phase_ref,
-    left_ref,
-    gather_ref,
-    cos_ref,
-    sin_ref,
-    near_ref,
-    fwd_ref,
-    done_ref,
-    mid,
-    spec,
-    turn,
-    outgoing,
-    incoming,
-    wide,
-    held,
-    pack_send,
-    pack_recv,
-    plane_send,
-    block_recv,
-    near_sem,
-):
+def column_kernel(dims, *refs):
+    sources = refs[:14]
+    gather_ref, cos_ref, sin_ref, near_ref, fwd_ref, done_ref = refs[14:20]
+    (
+        shift_ref,
+        offset_ref,
+        start_ref,
+        extent_ref,
+        slot_ref,
+        level_ref,
+        sig_ref,
+        shade_ref,
+        first_ref,
+        twiddle_ref,
+        second_ref,
+        back_ref,
+        phase_ref,
+    ) = refs[20:33]
+    weights, mid, spec, turn, outgoing, incoming, wide, held = refs[33:41]
+    pack_send, pack_recv, plane_send, block_recv, load_sem = refs[41:]
+    loads = [
+        pltpu.make_async_copy(source, target, load_sem.at[n])
+        for n, (source, target) in enumerate(zip(sources, refs[20:33]))
+    ]
+    loads.append(pltpu.make_async_copy(sources[13].at[lax.axis_index("facet")], near_ref, load_sem.at[13]))
+    order = [6, 7, 8, 9, 10, 0, 1, 2, 3, 4, 5, 11, 12, 13]
+    for n in order:
+        loads[n].start()
     facets, owners, teams, strip_rows, facet_len, grid_size, slots, total_subs = dims
     facet_id = lax.axis_index("facet")
     sub_id = lax.axis_index("sub")
@@ -190,9 +185,6 @@
     pl.semaphore_signal(barrier, inc=1, device_id=(facet_id, sub_id, sibling), device_id_type=MESH)
     peers += 1
 
-    near_copy = pltpu.make_async_copy(left_ref.at[facet_id], near_ref, near_sem)
-    near_copy.start()
-
     def holder(slot):
         def look(j, found):
             return jnp.where(slot_ref[j] == slot, j, found)
@@ -201,11 +193,17 @@
 
     outer_len = facet_len // LANES
     fold = LANES // outer_len
+    for n in order[:5]:
+        loads[n].wait()
     tw_cos = twiddle_ref[0]
     tw_sin = twiddle_ref[1]
 
+    for c in range(2):
+        weights[pl.ds(c, outer_len, stride=2), :] = shade_ref[...]
+
     def first_step(r, carry):
-        got = jnp.dot(first_ref[...], sig_ref[r], preferred_element_type=jnp.float32)
+        signal = sig_ref[r].reshape(2 * outer_len, LANES).astype(jnp.float32) * weights[...]
+        got = jnp.dot(first_ref[...], signal.astype(jnp.bfloat16), preferred_element_type=jnp.float32)
         real, imag = got[:outer_len], got[outer_len:]
         rows = pl.ds(pl.multiple_of(r * outer_len, outer_len), outer_len)
         mid[rows, :LANES] = (real * tw_cos - imag * tw_sin).astype(jnp.bfloat16)
@@ -232,6 +230,8 @@
 
     lax.fori_loop(0, strip_rows // fold, second_step, 0)
 
+    for n in range(6):
+        loads[n].wait()
     holders = [holder(p) for p in range(total_subs)]
     row_ids = lax.broadcasted_iota(jnp.int32, (total_subs, width), 0)
     k_ids = lax.broadcasted_iota(jnp.int32, (total_subs, width), 1)
@@ -255,8 +255,8 @@
     pieces = width // LANES
     my_slot = facet_id // group
     packs = []
-    order = [s for s in range(slots // 2, slots)] + [s for s in range(slots // 2)][::-1]
-    for step in order:
+    steps = [s for s in range(slots // 2, slots)] + [s for s in range(slots // 2)][::-1]
+    for step in steps:
         for turn_o in list(range(1, owners)) + [0]:
             slot = lax.rem(my_slot + step, slots)
             owner = lax.rem(sub_id + turn_o, owners)
@@ -314,6 +314,8 @@
                     copy.start()
                     packs.append((copy, True))
 
+    loads[11].wait()
+    loads[12].wait()
     for p in range(RADIX):
         wide[p, :part] = back_ref[p]
         wide[p, part:, :part] = -back_ref[p][:, part:]
@@ -397,7 +399,7 @@
     image = jnp.concatenate([jnp.concatenate(images[c], 1) for c in range(2)], 0).astype(jnp.bfloat16)
     for h in range(PARTS):
         gather_ref[facet_id, team_id, h] = image[h * piece_rows : (h + 1) * piece_rows]
-    near_copy.wait()
+    loads[13].wait()
 
     def send(kind, f, team, h, target):
         return pltpu.make_async_remote_copy(
@@ -547,7 +549,7 @@
             pl.when(away)(copy.wait_send)
 
 
-def column(scalars, sig, tables, left, phase, dims, layers, early):
+def column(scalars, sig, shade, tables, left, phase, dims, layers, early):
     facets, owners, teams, strip_rows, facet_len, grid_size, slots, total_subs = dims
     first, twiddle, second, back = [jnp.asarray(x) for x in tables]
     group = facets // slots
@@ -555,8 +557,9 @@
     width = grid_size // 2
     part = grid_size // RADIX
     band = phase.shape[0]
-    smem = pl.BlockSpec(memory_space=pltpu.SMEM)
+    hbm = pl.BlockSpec(memory_space=pltpu.HBM)
     vmem = pl.BlockSpec(memory_space=pltpu.VMEM)
+    operands = [*scalars, sig, shade, first, twiddle, second, back, phase]
     blocks = (facets, teams, PARTS, 2 * owners * chunk // PARTS, grid_size)
     spread = teams // 2
     return pl.pallas_call(
@@ -569,9 +572,12 @@
             jax.ShapeDtypeStruct((RADIX, 2 * part, 2 * part), jnp.bfloat16),
             jax.ShapeDtypeStruct((max(early, 1), layers, band if early else 16, 2, grid_size), jnp.bfloat16),
         ],
-        in_specs=[smem] * 6 + [vmem] * 6 + [pl.BlockSpec(memory_space=pl.ANY)],
+        in_specs=[hbm] * 14,
         out_specs=[vmem] * 6,
-        scratch_shapes=[
+        scratch_shapes=[pltpu.SMEM(x.shape, x.dtype) for x in operands[:6]]
+        + [pltpu.VMEM(x.shape, x.dtype) for x in operands[6:]]
+        + [
+            pltpu.VMEM((2 * facet_len // LANES, LANES), jnp.float32),
             pltpu.VMEM((strip_rows * (facet_len // LANES), 2 * LANES), jnp.bfloat16),
             pltpu.VMEM((2 * facet_len // LANES, strip_rows, LANES), jnp.float32),
             pltpu.VMEM((2, total_subs, 1, width), jnp.float32),
@@ -583,13 +589,13 @@
             pltpu.SemaphoreType.DMA((facets, owners)),
             pltpu.SemaphoreType.DMA((2 + spread, facets, spread, PARTS)),
             pltpu.SemaphoreType.DMA((facets, teams, PARTS)),
-            pltpu.SemaphoreType.DMA,
+            pltpu.SemaphoreType.DMA((14,)),
         ],
         compiler_params=pltpu.CompilerParams(
             collective_id=0, has_side_effects=True, vmem_limit_bytes=VMEM_COLUMN
         ),
         cost_estimate=pl.CostEstimate(flops=2_000_000_000, bytes_accessed=20_000_000, transcendentals=0),
-    )(*scalars, sig, first, twiddle, second, back, phase, left)
+    )(*[pltpu.with_memory_space_constraint(x, pltpu.HBM) for x in operands + [left]])
 
 
 def finish_kernel(early, facets, right_ref, cos_ref, sin_ref, near_ref, fwd_ref, done_ref, out_ref, held, ready, done_sem, ready_sem):
@@ -674,8 +680,8 @@
     dims = (facets, owners, teams, strip_rows, facet_len, grid_size, slots, total_subs)
 
     outer_len = facet_len // LANES
-    sig = (facet_data[0].astype(jnp.float32) * window).astype(jnp.bfloat16)
-    sig = sig.reshape(strip_rows, 2 * outer_len, LANES)
+    sig = facet_data[0].reshape(strip_rows, 2, outer_len, LANES).transpose(0, 2, 1, 3)
+    shade = window.reshape(outer_len, LANES)
     tables = strip_tables(facet_len, grid_size)
     scalars = (facet_shift, sub_offset, win_start, win_extent, owner_slot, layer_w)
     g_ids, t_ids, c_ids, o_ids, r_ids = np.meshgrid(
@@ -691,7 +697,7 @@
     left = jnp.asarray(left.reshape(facets, HALVES, 2 * band // HALVES, 2 * strip_total))
 
     early = facets - 1 if group == 1 and layers * HALVES == PARTS else 0
-    right, cos, sin, near, fwd, done = column(scalars, sig, tables, left, screen_phase, dims, layers, early)
+    right, cos, sin, near, fwd, done = column(scalars, sig, shade, tables, left, screen_phase, dims, layers, early)
     if not early:
         right = right.reshape(slots, 2 * strip_total, grid_size)
     return finish(right, cos, sin, near, fwd, done, early, facets)

time: 46.7 us -> 41.9 us (0.90)
  local copies, waits for them, and re-layouts: 4.24 us -> 0 us
  other arithmetic: 1.34 us -> 0 us
  Pallas kernels: 40.7 us -> 41.8 us
    convert_element_type x1 -> x0, local copies, waits for them, and re-layouts: 2.45 us -> none  [local(): sig = (facet_data[0].astype(jnp.float32) * window).astype(jnp.bfloat16)]
    convert_element_type x1 -> x0, other arithmetic: 1.34 us -> none  [local(): sig = (facet_data[0].astype(jnp.float32) * window).astype(jnp.bfloat16)]
    pallas_call x1, Pallas kernels: 36.6 us -> 37.6 us  [column(): pl.pallas_call(functools.partial(column_kernel, dims), out_shape=[jax.Sha...]
    mul x1 -> x0, local copies, waits for them, and re-layouts: 0.91 us -> none  [local(): sig = (facet_data[0].astype(jnp.float32) * window).astype(jnp.bfloat16)]
    unnamed x24 -> x0, local copies, waits for them, and re-layouts: 0.88 us -> none
where the time goes in v3:
time: 41.9 us; the launch traced here: 41.8 us
  Pallas kernels  41.8 us (100%)
    pallas_call x1, Pallas kernels, column(): pl.pallas_call(functools.partial(column_kernel, dims), out_shape=[jax.Sha...  37.6 us
    pallas_call x1, Pallas kernels, finish(): pl.pallas_call(functools.partial(finish_kernel, early, facets), out_shape...  4.16 us

profile of v3, /device:TPU:0, one launch (start us, length us, event | category | flops | bytes accessed | tf_op | source)
XLA Modules:
  0.0 41.8 jit_solution(10209521125166590774)
XLA Ops:
  0.0 37.6 %shard_map.136 = (bf16[4,4,4,16,1024]{4,3,2,1,0:T(8,128)(2,1)S(1)}, f32[2,256,1024]{2,1,0:T(8,128)S(1)}, f32[2,256,1024]{2,1,0:T(8,128)S(1)}, bf16[2,256,256]{2,...) custom-call(s32[4]{0:T(128)} %refs_0_.1, s32[8]{0:T(128)} %refs_1_.1, ...), custom_call_target="tpu_custom_call" | custom-call | flops 2000000000 | bytes 20000000 | tf_op jit(solution)/shard_map/pallas_call | solution.py:565
  37.6 4.2 %shard_map.137 = bf16[4,2,256,2,1024]{4,3,2,1,0:T(2,128)(2,1)} custom-call(bf16[4,4,4,16,1024]{4,3,2,1,0:T(8,128)(2,1)S(1)} %get-tuple-element.11.right_ref, f32[2,256,1024]{2,1,0:T(8,128)S(1)} %get-tuple-element.12.cos_ref, f32[2,256,1024]{2,1,0:T(8,128)S(1)} %get-tuple-element.13.sin_ref, bf16[2,256,256]{2,1,0:T(8,128)(2,1)S(1)} %get-tuple-element.14.near_ref, ...), custom_call_target="tpu_custom_call" | custom-call | flops 2000000000 | bytes 20000000 | tf_op jit(solution)/shard_map/pallas_call | solution.py:641

commit v4 on v3

--- a/solution.py
+++ b/solution.py
@@ -139,8 +139,8 @@
         back_ref,
         phase_ref,
     ) = refs[20:33]
-    weights, mid, spec, turn, outgoing, incoming, wide, held = refs[33:41]
-    pack_send, pack_recv, plane_send, block_recv, load_sem = refs[41:]
+    weights, mid, spec, turn, outgoing, incoming, wide, held, keeper = refs[33:42]
+    pack_send, pack_recv, plane_send, block_recv, load_sem = refs[42:]
     loads = [
         pltpu.make_async_copy(source, target, load_sem.at[n])
         for n, (source, target) in enumerate(zip(sources, refs[20:33]))
@@ -185,11 +185,16 @@
     pl.semaphore_signal(barrier, inc=1, device_id=(facet_id, sub_id, sibling), device_id_type=MESH)
     peers += 1
 
+    def look(j, slot, found):
+        return jnp.where(slot_ref[j] == slot, j, found)
+
     def holder(slot):
-        def look(j, found):
-            return jnp.where(slot_ref[j] == slot, j, found)
-
-        return lax.fori_loop(0, total_subs, look, jnp.int32(0))
+        if total_subs > 8:
+            return lax.fori_loop(0, total_subs, lambda j, found: look(j, slot, found), jnp.int32(0))
+        found = jnp.int32(0)
+        for j in range(total_subs):
+            found = look(j, slot, found)
+        return found
 
     outer_len = facet_len // LANES
     fold = LANES // outer_len
@@ -201,21 +206,21 @@
     for c in range(2):
         weights[pl.ds(c, outer_len, stride=2), :] = shade_ref[...]
 
-    def first_step(r, carry):
+    def first_step(r):
         signal = sig_ref[r].reshape(2 * outer_len, LANES).astype(jnp.float32) * weights[...]
         got = jnp.dot(first_ref[...], signal.astype(jnp.bfloat16), preferred_element_type=jnp.float32)
         real, imag = got[:outer_len], got[outer_len:]
-        rows = pl.ds(pl.multiple_of(r * outer_len, outer_len), outer_len)
+        rows = slice(r * outer_len, (r + 1) * outer_len)
         mid[rows, :LANES] = (real * tw_cos - imag * tw_sin).astype(jnp.bfloat16)
         mid[rows, LANES:] = (real * tw_sin + imag * tw_cos).astype(jnp.bfloat16)
-        return carry
-
-    lax.fori_loop(0, strip_rows, first_step, 0)
+
+    for r in range(strip_rows):
+        first_step(r)
     tall = LANES // fold
     lane = lax.broadcasted_iota(jnp.int32, (tall, LANES), 1)
 
-    def second_step(i, carry):
-        rows = pl.ds(pl.multiple_of(i * LANES, LANES), LANES)
+    def second_step(i):
+        rows = slice(i * LANES, (i + 1) * LANES)
         got = lax.dot_general(
             second_ref[...], mid[rows, :], (((1,), (1,)), ((), ())), preferred_element_type=jnp.float32
         )
@@ -226,13 +231,15 @@
             far = jnp.where(lane < outer_len, pltpu.roll(even, outer_len, 1), odd)
             spec[c * tall : (c + 1) * tall, i * fold, :] = near
             spec[c * tall : (c + 1) * tall, i * fold + 1, :] = far
-        return carry
-
-    lax.fori_loop(0, strip_rows // fold, second_step, 0)
+
+    for i in range(strip_rows // fold):
+        second_step(i)
 
     for n in range(6):
         loads[n].wait()
     holders = [holder(p) for p in range(total_subs)]
+    for p in range(total_subs):
+        keeper[p] = holders[p]
     row_ids = lax.broadcasted_iota(jnp.int32, (total_subs, width), 0)
     k_ids = lax.broadcasted_iota(jnp.int32, (total_subs, width), 1)
     starts = jnp.zeros((total_subs, width), jnp.int32)
@@ -256,12 +263,12 @@
     my_slot = facet_id // group
     packs = []
     steps = [s for s in range(slots // 2, slots)] + [s for s in range(slots // 2)][::-1]
-    for step in steps:
-        for turn_o in list(range(1, owners)) + [0]:
+    for turn_o in range(owners):
+        for step in steps:
             slot = lax.rem(my_slot + step, slots)
             owner = lax.rem(sub_id + turn_o, owners)
             p = owner * slots + slot
-            j = holder(p)
+            j = keeper[p]
             begin = lax.rem(offset_ref[j] + start_ref[facet_id, j], facet_len)
             q0 = lax.div(begin, LANES)
             shift = begin - q0 * LANES
@@ -321,7 +328,7 @@
         wide[p, part:, :part] = -back_ref[p][:, part:]
         wide[p, part:, part:] = back_ref[p][:, :part]
         fwd_ref[p] = wide[p].T
-    mine = holder(sub_id * slots + my_slot)
+    mine = keeper[sub_id * slots + my_slot]
     f_rows = lax.broadcasted_iota(jnp.int32, (facets, grid_size), 0)
     at = lax.broadcasted_iota(jnp.int32, (facets, grid_size), 1)
     v_ids = (at % part) * RADIX + at // part
@@ -356,8 +363,10 @@
                 cos_ref[l, :, lanes] = cos
                 sin_ref[l, :, lanes] = sin
 
-    for off in range(facets):
-        for turn_o in range(owners):
+    staged = PARTS == 2 * owners and group == 1
+
+    def received(turn_o):
+        for off in range(facets):
             if off or turn_o:
                 f = lax.rem(facet_id + off, facets)
                 o = lax.rem(sub_id + turn_o, owners)
@@ -370,36 +379,54 @@
                     device_id_type=MESH,
                 ).wait_recv()
 
-    got = incoming[...].reshape(facets * owners * chunk, 2 * width).astype(jnp.float32)
-    low_r, high_r = got[:, :part], got[:, part:width]
-    low_i, high_i = got[:, width : width + part], got[:, width + part :]
-    rows_f = owners * chunk
-    images = [[], []]
-    for p in range(RADIX):
-        real, imag = [
-            (low_r + high_r, low_i + high_i),
-            (low_r - high_i, low_i + high_r),
-            (low_r - high_r, low_i - high_i),
-            (low_r + high_i, low_i - high_r),
-        ][p]
-        pair = jnp.concatenate([real.astype(jnp.bfloat16), imag.astype(jnp.bfloat16)], 1)
-        moved = jnp.dot(pair, wide[p], preferred_element_type=jnp.float32)
-        total_r = jnp.zeros((rows_f, part), jnp.float32)
-        total_i = jnp.zeros((rows_f, part), jnp.float32)
-        for f in range(facets):
-            cos = ramp_cos[f : f + 1, p * part : (p + 1) * part]
-            sin = ramp_sin[f : f + 1, p * part : (p + 1) * part]
-            real = moved[f * rows_f : (f + 1) * rows_f, :part]
-            imag = moved[f * rows_f : (f + 1) * rows_f, part:]
-            total_r = total_r + (real * cos - imag * sin)
-            total_i = total_i + (real * sin + imag * cos)
-        images[0].append(total_r)
-        images[1].append(total_i)
-    piece_rows = 2 * rows_f // PARTS
-    image = jnp.concatenate([jnp.concatenate(images[c], 1) for c in range(2)], 0).astype(jnp.bfloat16)
-    for h in range(PARTS):
-        gather_ref[facet_id, team_id, h] = image[h * piece_rows : (h + 1) * piece_rows]
-    loads[13].wait()
+    def imaged(got, rows_f):
+        got = got.astype(jnp.float32)
+        low_r, high_r = got[:, :part], got[:, part:width]
+        low_i, high_i = got[:, width : width + part], got[:, width + part :]
+        images = [[], []]
+        for p in range(RADIX):
+            real, imag = [
+                (low_r + high_r, low_i + high_i),
+                (low_r - high_i, low_i + high_r),
+                (low_r - high_r, low_i - high_i),
+                (low_r + high_i, low_i - high_r),
+            ][p]
+            pair = jnp.concatenate([real.astype(jnp.bfloat16), imag.astype(jnp.bfloat16)], 1)
+            moved = jnp.dot(pair, wide[p], preferred_element_type=jnp.float32)
+            total_r = jnp.zeros((rows_f, part), jnp.float32)
+            total_i = jnp.zeros((rows_f, part), jnp.float32)
+            for f in range(facets):
+                cos = ramp_cos[f : f + 1, p * part : (p + 1) * part]
+                sin = ramp_sin[f : f + 1, p * part : (p + 1) * part]
+                real = moved[f * rows_f : (f + 1) * rows_f, :part]
+                imag = moved[f * rows_f : (f + 1) * rows_f, part:]
+                total_r = total_r + (real * cos - imag * sin)
+                total_i = total_i + (real * sin + imag * cos)
+            images[0].append(total_r)
+            images[1].append(total_i)
+        return [jnp.concatenate(images[c], 1).astype(jnp.bfloat16) for c in range(2)]
+
+    def make_part(stage):
+        if staged:
+            received(stage)
+            o = lax.rem(sub_id + stage, owners)
+            got = jnp.concatenate([incoming[f, o] for f in range(facets)], 0)
+            images = imaged(got, chunk)
+            for c in range(2):
+                gather_ref[facet_id, team_id, c * owners + o] = images[c]
+        else:
+            for turn_o in range(owners):
+                received(turn_o)
+            got = incoming[...].reshape(facets * owners * chunk, 2 * width)
+            image = jnp.concatenate(imaged(got, owners * chunk), 0)
+            piece_rows = 2 * owners * chunk // PARTS
+            for h in range(PARTS):
+                gather_ref[facet_id, team_id, h] = image[h * piece_rows : (h + 1) * piece_rows]
+
+    def part_at(i):
+        if staged:
+            return lax.rem(i, 2) * owners + lax.rem(sub_id + lax.div(i, 2), owners)
+        return i
 
     def send(kind, f, team, h, target):
         return pltpu.make_async_remote_copy(
@@ -475,12 +502,12 @@
         for step in range(spread):
             arrive(f, lax.rem(sibling + cores * step, teams), h)
 
-    def each_part(body):
-        def run(h, carry):
-            body(h)
+    def each_part(body, first=0, last=PARTS):
+        def run(i, carry):
+            body(part_at(i))
             return carry
 
-        lax.fori_loop(0, PARTS, run, 0)
+        lax.fori_loop(first, last, run, 0)
 
     sequence = arrivals(facets, facet_id)
     early = facets - 1 if done_ref.shape[2] == cos_ref.shape[1] else 0
@@ -491,27 +518,34 @@
         across(facet_id, h, start)
         aside(facet_id, team_id, h, start)
 
-    each_part(own)
-
     def neighbours(h):
         from_below(1, h)
         from_above(1, h)
         partner(facet_id, h)
 
-    each_part(neighbours)
+    stages = owners if staged else 1
+    for stage in range(stages):
+        make_part(stage)
+        if stage == 0:
+            loads[13].wait()
+        span = PARTS // stages
+        each_part(own, stage * span, (stage + 1) * span)
+        each_part(neighbours, stage * span, (stage + 1) * span)
     each_part(late_across)
     each_part(lambda h: settled(sequence[0], h))
     for k in range(facets - 1):
 
-        def relay(h, k=k):
+        def relay(i, carry, k=k):
+            h = part_at(i)
             if k + 2 < facets:
                 from_below(k + 2, h)
                 from_above(k + 2, h)
             partner(sequence[k + 1], h)
             if k < early:
-                unit(h, gather_ref, sequence[k], near_ref, fwd_ref, cos_ref, sin_ref, held, done_ref.at[k])
-
-        each_part(relay)
+                unit(i, gather_ref, sequence[k], near_ref, fwd_ref, cos_ref, sin_ref, held, done_ref.at[k])
+            return carry
+
+        lax.fori_loop(0, PARTS, relay, 0)
         each_part(lambda h, k=k: settled(sequence[k + 1], h))
 
     def drain(h):
@@ -585,6 +619,7 @@
             pltpu.VMEM((facets, owners, chunk, 2 * width), jnp.bfloat16),
             pltpu.VMEM((RADIX, 2 * part, 2 * part), jnp.bfloat16),
             pltpu.VMEM((2 * band // HALVES, grid_size), jnp.bfloat16),
+            pltpu.SMEM((total_subs,), jnp.int32),
             pltpu.SemaphoreType.DMA((facets * owners,)),
             pltpu.SemaphoreType.DMA((facets, owners)),
             pltpu.SemaphoreType.DMA((2 + spread, facets, spread, PARTS)),

time: 41.9 us -> 39.1 us (0.933)
  Pallas kernels: 41.8 us -> 39 us
    pallas_call x1, Pallas kernels: 37.6 us -> 34.8 us  [column(): pl.pallas_call(functools.partial(column_kernel, dims), out_shape=[jax.Sha...]
where the time goes in v4:
time: 39.1 us; the launch traced here: 39 us
  Pallas kernels  39 us (100%)
    pallas_call x1, Pallas kernels, column(): pl.pallas_call(functools.partial(column_kernel, dims), out_shape=[jax.Sha...  34.8 us
    pallas_call x1, Pallas kernels, finish(): pl.pallas_call(functools.partial(finish_kernel, early, facets), out_shape...  4.15 us

profile of v4, /device:TPU:0, one launch (start us, length us, event | category | flops | bytes accessed | tf_op | source)
XLA Modules:
  0.0 39.0 jit_solution(18224783912255796063)
XLA Ops:
  0.0 34.8 %shard_map.136 = (bf16[4,4,4,16,1024]{4,3,2,1,0:T(8,128)(2,1)S(1)}, f32[2,256,1024]{2,1,0:T(8,128)S(1)}, f32[2,256,1024]{2,1,0:T(8,128)S(1)}, bf16[2,256,256]{2,...) custom-call(s32[4]{0:T(128)} %refs_0_.1, s32[8]{0:T(128)} %refs_1_.1, ...), custom_call_target="tpu_custom_call" | custom-call | flops 2000000000 | bytes 20000000 | tf_op jit(solution)/shard_map/pallas_call | solution.py:599
  34.8 4.2 %shard_map.137 = bf16[4,2,256,2,1024]{4,3,2,1,0:T(2,128)(2,1)} custom-call(bf16[4,4,4,16,1024]{4,3,2,1,0:T(8,128)(2,1)S(1)} %get-tuple-element.11.right_ref, f32[2,256,1024]{2,1,0:T(8,128)S(1)} %get-tuple-element.12.cos_ref, f32[2,256,1024]{2,1,0:T(8,128)S(1)} %get-tuple-element.13.sin_ref, bf16[2,256,256]{2,1,0:T(8,128)(2,1)S(1)} %get-tuple-element.14.near_ref, ...), custom_call_target="tpu_custom_call" | custom-call | flops 2000000000 | bytes 20000000 | tf_op jit(solution)/shard_map/pallas_call | solution.py:676

commit v5 on v4

--- a/solution.py
+++ b/solution.py
@@ -507,7 +507,7 @@
             body(part_at(i))
             return carry
 
-        lax.fori_loop(first, last, run, 0)
+        lax.fori_loop(first, last, run, 0, unroll=True)
 
     sequence = arrivals(facets, facet_id)
     early = facets - 1 if done_ref.shape[2] == cos_ref.shape[1] else 0
@@ -662,7 +662,7 @@
             ship(sequence[k], step).start()
             return carry
 
-        lax.fori_loop(0, layers * HALVES, run, 0)
+        lax.fori_loop(0, layers * HALVES, run, 0, unroll=True)
     for step in range(layers * HALVES):
         ship(sequence[slots - 1], step).wait()
     for copy in moved:

time: 39.1 us -> 38.8 us (level)
  Pallas kernels: 39 us -> 38.5 us
where the time goes in v5:
time: 38.8 us; the launch traced here: 38.6 us
  Pallas kernels  38.5 us (99%)
    pallas_call x1, Pallas kernels, column(): pl.pallas_call(functools.partial(column_kernel, dims), out_shape=[jax.Sha...  34.7 us
    pallas_call x1, Pallas kernels, finish(): pl.pallas_call(functools.partial(finish_kernel, early, facets), out_shape...  3.78 us

profile of v5, /device:TPU:0, one launch (start us, length us, event | category | flops | bytes accessed | tf_op | source)
XLA Modules:
  0.0 38.6 jit_solution(11072890941851526857)
XLA Ops:
  0.0 34.7 %shard_map.136 = (bf16[4,4,4,16,1024]{4,3,2,1,0:T(8,128)(2,1)S(1)}, f32[2,256,1024]{2,1,0:T(8,128)S(1)}, f32[2,256,1024]{2,1,0:T(8,128)S(1)}, bf16[2,256,256]{2,...) custom-call(s32[4]{0:T(128)} %refs_0_.1, s32[8]{0:T(128)} %refs_1_.1, ...), custom_call_target="tpu_custom_call" | custom-call | flops 2000000000 | bytes 20000000 | tf_op jit(solution)/shard_map/pallas_call | solution.py:599
  34.7 3.8 %shard_map.137 = bf16[4,2,256,2,1024]{4,3,2,1,0:T(2,128)(2,1)} custom-call(bf16[4,4,4,16,1024]{4,3,2,1,0:T(8,128)(2,1)S(1)} %get-tuple-element.11.right_ref, f32[2,256,1024]{2,1,0:T(8,128)S(1)} %get-tuple-element.12.cos_ref, f32[2,256,1024]{2,1,0:T(8,128)S(1)} %get-tuple-element.13.sin_ref, bf16[2,256,256]{2,1,0:T(8,128)(2,1)S(1)} %get-tuple-element.14.near_ref, ...), custom_call_target="tpu_custom_call" | custom-call | flops 2000000000 | bytes 20000000 | tf_op jit(solution)/shard_map/pallas_call | solution.py:676
